TPU v7x, 32 devices: a whole 2x2x4 slice. The times are simulated.
32 devices in a mesh: role: 4 (over y, x), ep: 4 (over z), dp: 2 (over core).
Axes of the slice: x: 2, y: 2, z: 4, core: 2. Of those that a mesh axis runs over, the one named last changes fastest.
Arguments:
- latents: bfloat16 [16, 256, 1536], P(('role', 'dp'), 'ep'), may hold values from -6 to 6
- noise: bfloat16 [1, 16, 256, 1536], P(None, ('role', 'dp'), 'ep'), may hold values from -6 to 6
- expert_ids: int32 [1, 16, 256, 6], P(None, ('role', 'dp'), 'ep'), may hold values from 0 to 63, all different within a row; in each aligned block of 64 rows (0 to 63, 64 to 127, ..., all dimensions but the last counted through in order) at most 7 rows name the same one
- gate_values: float32 [1, 16, 256, 6], P(None, ('role', 'dp'), 'ep'), may hold values from 0.1 to 1
- advantages: float32 [16], P(('role', 'dp')), may hold values from -4 to 4
- expert_pair: bfloat16 [64, 2, 768, 1536], P('ep', None, ('role', 'dp')), may hold values from -6 to 6
Outputs:
- final_latents: bfloat16 [16, 256, 1536], P(('role', 'dp'), 'ep')
- new_down: bfloat16 [64, 768, 1536], P('ep')
Inputs may be any that keep to these rules, and one draw needn't show every extreme that they name: `expert_ids`: each row names 6 different experts. In every aligned block of 64 rows (steps, images and tokens taken together in order; one index of ep holds one block of an image at a step) no expert is named more than 7 times, a bound that some block reaches.
All inputs are finite; a program needn't handle non-finite values.
Results may differ from a plain program's by a relative error of at most 0.008.
Values may be sent and summed in bfloat16 or wider, within the bound.
No kernel may reach another device: no remote copies, remote signals or barrier semaphores. Data moves between devices by JAX's collectives and lax.ppermute only.
A program may use at most 256 MiB of HBM per device.

v0:
```python
import math

import jax
import jax.numpy as jnp
from jax import lax
from jax.sharding import PartitionSpec as P

CAP = 7


def coefficients(section):
    moment = 0.95 - 0.4 * section
    noise_level = 0.3 * math.sqrt(moment / (1.0 - moment))
    factor = noise_level * noise_level / (2.0 * moment)
    keep_gain = 1.0 - 0.4 * factor
    drift_gain = -0.4 * (1.0 + factor * (1.0 - moment))
    noise_gain = noise_level * math.sqrt(0.4)
    return (keep_gain, drift_gain, noise_gain)


def slot_matrices(picked, weights, experts, capacity):
    image_count, tokens, chosen_count = picked.shape
    flat_ids = picked.reshape(image_count, tokens * chosen_count)
    onehot = (flat_ids[..., None] == jnp.arange(experts, dtype=jnp.int32)).astype(jnp.int32)
    ranks = jnp.cumsum(onehot, axis=1) - 1
    placed = jnp.sum(ranks * onehot, axis=2)
    image_column = jnp.arange(image_count, dtype=jnp.int32)[:, None]
    slot_ids = (flat_ids * image_count + image_column) * capacity + placed
    slot_ids = slot_ids.reshape(image_count * tokens, chosen_count)
    total_slots = experts * image_count * capacity
    marked = (slot_ids[..., None] == jnp.arange(total_slots, dtype=jnp.int32)).astype(jnp.float32)
    selected = jnp.sum(marked, axis=1)
    flat_weights = weights.reshape(image_count * tokens, chosen_count)
    slot_gate = jnp.sum(jnp.sum(marked * flat_weights[..., None], axis=1), axis=0)
    return (slot_ids, selected, slot_gate, flat_weights)


def expert_pass(inputs, w_up, w_down):
    width = inputs.shape[-1]
    hidden_units = w_up.shape[1]
    pre_act = jnp.einsum("jlcd,lhd->jlch", inputs, w_up, preferred_element_type=jnp.float32) * (
        1.0 / math.sqrt(width)
    )
    hidden = jax.nn.gelu(pre_act, approximate=True).astype(jnp.bfloat16)
    output = jnp.einsum("jlch,lhd->jlcd", hidden, w_down, preferred_element_type=jnp.float32) * (
        1.0 / math.sqrt(hidden_units)
    )
    returned = lax.all_to_all(
        output.astype(jnp.bfloat16), "ep", split_axis=0, concat_axis=0, tiled=True
    )
    return (returned, hidden)


def per_device(latents, noise, expert_ids, gate_values, advantages, expert_pair):
    ep_size = lax.axis_size("ep")
    group_size = lax.axis_size("role") * lax.axis_size("dp")
    local_experts = expert_pair.shape[0]
    experts = local_experts * ep_size
    capacity = CAP
    image_count = latents.shape[0]
    tok_count = latents.shape[1]
    width = latents.shape[2]
    top_count = expert_ids.shape[3]
    total_slots = experts * image_count * capacity
    full_pair = lax.all_gather(expert_pair, ("role", "dp"), axis=2, tiled=True)
    w_up = full_pair[:, 0]
    w_down = full_pair[:, 1]
    hidden_units = full_pair.shape[2]
    current = latents.reshape(image_count * tok_count, width)
    image_of_slot = jnp.arange(total_slots, dtype=jnp.int32) // capacity % image_count
    keep_gain, drift_gain, noise_gain = coefficients(0)
    slot_ids, selected, slot_gate, flat_weights = slot_matrices(
        expert_ids[0], gate_values[0], experts, capacity
    )
    selected_half = selected.astype(jnp.bfloat16)
    noise_now = noise[0].reshape(image_count * tok_count, width)
    slot_latent = jnp.einsum(
        "ts,td->sd", selected_half, current, preferred_element_type=jnp.float32
    )
    slot_latent = slot_latent.astype(jnp.bfloat16).reshape(
        ep_size, local_experts, image_count * capacity, width
    )
    slot_noise = jnp.einsum(
        "ts,td->sd", selected_half, noise_now, preferred_element_type=jnp.float32
    )
    image_factor = advantages * (drift_gain / noise_gain)
    slot_scale = slot_gate * image_factor[image_of_slot]
    home_cot = (
        (slot_scale[:, None] * slot_noise)
        .astype(jnp.bfloat16)
        .reshape(ep_size, local_experts, image_count * capacity, width)
    )
    returned, hidden = expert_pass(
        lax.all_to_all(slot_latent, "ep", split_axis=0, concat_axis=0, tiled=True), w_up, w_down
    )
    returned, hidden, cotangent = (
        returned,
        hidden,
        lax.all_to_all(home_cot, "ep", split_axis=0, concat_axis=0, tiled=True),
    )
    back_rows = returned.reshape(total_slots, width)
    taken = jnp.take(back_rows, slot_ids, axis=0)
    velocity = jnp.sum(flat_weights[..., None] * taken.astype(jnp.float32), axis=1)
    moved = (
        keep_gain * current.astype(jnp.float32)
        + drift_gain * velocity
        + noise_gain * noise_now.astype(jnp.float32)
    )
    current = moved.astype(jnp.bfloat16)
    kept_hidden = [hidden]
    kept_cot = [cotangent]
    rate = 10.0 / math.sqrt(tok_count * ep_size * top_count * image_count * group_size / experts)
    share_rows = expert_pair.shape[2]
    total = jnp.zeros(
        (lax.axis_size(("role", "dp")) * share_rows, local_experts, width), jnp.float32
    )
    for hidden, cotangent in zip(kept_hidden, kept_cot):
        total = jnp.einsum("jlch,jlcd->hld", hidden, cotangent, preferred_element_type=jnp.float32)
    share = lax.psum_scatter(
        (total * (1.0 / math.sqrt(hidden_units)))
        .reshape(lax.axis_size(("role", "dp")) * share_rows, local_experts * width)
        .astype(jnp.bfloat16),
        ("role", "dp"),
        scatter_dimension=0,
        tiled=True,
    ).astype(jnp.float32)
    share = jnp.transpose(share.reshape(share_rows, local_experts, width), (1, 0, 2))
    own_down = expert_pair[:, 1].astype(jnp.float32)
    new_part = (own_down + rate * share).astype(jnp.bfloat16)
    new_down = lax.all_gather(new_part, ("role", "dp"), axis=1, tiled=True)
    return (current.reshape(image_count, tok_count, width), new_down)


def solution(mesh):
    in_specs = (
        P(("role", "dp"), "ep", None),
        P(None, ("role", "dp"), "ep", None),
        P(None, ("role", "dp"), "ep", None),
        P(None, ("role", "dp"), "ep", None),
        P(("role", "dp")),
        P("ep", None, ("role", "dp"), None),
    )
    out_specs = (P(("role", "dp"), "ep", None), P("ep", None, None))
    return jax.shard_map(
        per_device, mesh=mesh, in_specs=in_specs, out_specs=out_specs, check_vma=False
    )
```

profile of v0, /device:TPU:0, one launch (start us, length us, event | category | flops | bytes accessed | tf_op | source)
XLA Modules:
  0.0 899.5 jit_solution(12513486669009468954)
XLA Ops:
  7.2 8.4 copy.82
  16.8 1.8 reduce-window.6
  20.0 2.4 convolution_convert_fusion
  22.5 3.9 reshape.233
  26.4 3.6 copy.81
  30.0 6.6 all-to-all-start
  37.2 1.4 fusion.23
  38.6 2.7 multiply_convert_fusion.1
  41.3 4.1 reshape.235
  45.4 3.0 copy.89
  48.4 50.5 %all-to-all-done = bf16[4,16,14,1536]{3,1,2,0:T(8,128)(2,1)} async-done(((bf16[4,16,14,1536]{3,1,2,0:T(8,128)(2,1)}), bf16[4,16,14,1536]{3,1,2,0:T(8,128)(2,1)}, u32[]{:S(2)}, u32[]{:S(2)}) %all-to-all-start) | async-done | bytes 2752544 | tf_op jit(solution)/shard_map/all_to_all | solution.py:94
  99.0 3.7 all-to-all-start.2
  102.8 254.7 %all-gather.3.cloned.1.call-done = bf16[16,2,768,1536]{3,2,0,1:T(8,128)(2,1)} async-done(((bf16[16,2,96,1536]{3,2,0,1:T(8,128)(2,1)}), bf16[16,2,768,1536]{3,2,0,1:T(8,128)(2,1)}) %all-gather.3.cloned.1.call-update) | async-done | bytes 75497488 | tf_op jit(solution)/shard_map/all_gather | solution.py:65
  357.5 19.1 %fusion.12 = bf16[4,16,14,768]{3,2,0,1:T(8,128)(2,1)} fusion(bf16[16,2,768,1536]{3,2,0,1:T(8,128)(2,1)} %all-gather.3.cloned.1.call-done, bf16[4,16,14,1536]{3,1,2,0:T(8,128)(2,1)} %all-to-all-done), kind=kOutput, calls=%fused_computation.24 | convolution fusion | flops 2120810496 | bytes 41877504 | tf_op jit(solution)/shard_map/jlcd,lhd->jlch/dot_general | solution.py:41
  376.6 18.7 %fusion = bf16[16,1536,768]{2,1,0:T(8,128)(2,1)} fusion(bf16[4,16,14,768]{3,2,0,1:T(8,128)(2,1)} %fusion.12, bf16[4,16,14,1536]{3,1,2,0:T(8,128)(2,1)S(1)} %all-to-all-done.2), kind=kOutput, calls=%fused_computation.2 | convolution fusion | flops 2151677952 | bytes 41877504 | tf_op jit(solution)/shard_map/jlch,jlcd->hld/dot_general | solution.py:118
  395.3 48.6 %copy.91 = bf16[768,24576]{1,0:T(8,128)(2,1)} copy(bf16[768,24576]{0,1:T(8,128)(2,1)} %bitcast.85) | data formatting | bytes 75497472 | tf_op jit(solution)/shard_map/convert_element_type | solution.py:122
  444.2 4.9 slice.19
  449.1 220.6 %reduce-scatter.2.cloned.1.call-done = bf16[96,24576]{1,0:T(8,128)(2,1)} async-done(((bf16[768,24576]{1,0:T(8,128)(2,1)}), bf16[96,24576]{1,0:T(8,128)(2,1)}) %reduce-scatter.2.cloned.1.call-update) | async-done | bytes 4718608 | tf_op jit(solution)/shard_map/reduce_scatter | solution.py:119
  669.7 3.3 convert_multiply_fusion
  673.1 6.5 copy.98
  679.5 7.4 fusion.3
  688.4 19.8 %fusion.4 = bf16[4,16,14,1536]{3,2,0,1:T(8,128)(2,1)S(1)} fusion(bf16[4,16,14,768]{3,2,0,1:T(8,128)(2,1)S(1)} %copy-done.7, bf16[16,2,768,1536]{3,2,0,1:T(8,128)(2,1)} %all-gather.3.cloned.1.call-done), kind=kOutput, calls=%fused_computation.16 | convolution fusion | flops 2116681728 | bytes 41877504 | tf_op jit(solution)/shard_map/jlch,lhd->jlcd/dot_general | solution.py:45
  708.2 3.0 copy.84
  711.2 4.4 all-to-all-start.1
  716.5 60.8 %all-to-all-done.1 = bf16[4,16,14,1536]{3,1,2,0:T(8,128)(2,1)S(1)} async-done(((bf16[4,16,14,1536]{3,1,2,0:T(8,128)(2,1)}), bf16[4,16,14,1536]{3,1,2,0:T(8,128)(2,1)S(1)}, u32[]{:S(2)}, u32[]{:S(2)}) %all-to-all-start.1) | async-done | bytes 2752544 | tf_op jit(solution)/shard_map/all_to_all | solution.py:48
  777.3 3.2 copy.85
  780.5 3.8 reshape.234
  784.3 3.8 gather_fusion
  788.1 3.7 reshape.238
  791.8 3.2 multiply_reduce_fusion
  796.0 70.6 %all-gather.5.cloned.1.call-done = bf16[16,768,1536]{2,0,1:T(8,128)(2,1)} async-done(((bf16[16,96,1536]{2,0,1:T(8,128)(2,1)}), bf16[16,768,1536]{2,0,1:T(8,128)(2,1)}) %all-gather.5.cloned.1.call-update) | async-done | bytes 37748752 | tf_op jit(solution)/shard_map/all_gather | solution.py:130
  866.6 25.9 %copy.92 = bf16[16,768,1536]{2,1,0:T(8,128)(2,1)} copy(bf16[16,768,1536]{2,0,1:T(8,128)(2,1)} %all-gather.5.cloned.1.call-done) | data formatting | bytes 75497472
  (56 shorter events, 6.9 us)
Async XLA Ops:
  7.2 350.3 %all-gather.3.cloned.1.call-start = ((), (), s32[]{:S(2)}) async-start(), calls=%async_computation.4 | async-start | bytes 84934656 | tf_op jit(solution)/shard_map/all_gather | solution.py:65
  15.6 0.7 copy-start.4
  15.6 1.1 copy-start.5
  15.6 4.4 copy-start.2
  30.0 6.6 copy-start.6
  30.0 8.6 copy-start
  30.0 69.0 %all-to-all-start = ((bf16[4,16,14,1536]{3,1,2,0:T(8,128)(2,1)}), bf16[4,16,14,1536]{3,1,2,0:T(8,128)(2,1)}, u32[]{:S(2)}, u32[]{:S(2)}) async-start(bf16[4,16,14,1536]{3,1,2,0:T(8,128)(2,1)} %copy.81), calls=%async_computation | async-start | bytes 5505024 | tf_op jit(solution)/shard_map/all_to_all | solution.py:94
  99.0 277.6 %all-to-all-start.2 = ((bf16[4,16,14,1536]{3,1,2,0:T(8,128)(2,1)}), bf16[4,16,14,1536]{3,1,2,0:T(8,128)(2,1)S(1)}, u32[]{:S(2)}, u32[]{:S(2)}) async-start(bf16[4,16,14,1536]{3,1,2,0:T(8,128)(2,1)} %copy.89), calls=%async_computation.2 | async-start | bytes 5505024 | tf_op jit(solution)/shard_map/all_to_all | solution.py:99
  102.6 567.1 %reduce-scatter.2.cloned.1.call-start = ((), (), s32[]{:S(2)}) async-start(), calls=%async_computation.5 | async-start | bytes 42467328 | tf_op jit(solution)/shard_map/reduce_scatter | solution.py:119
  443.9 422.7 %all-gather.5.cloned.1.call-start = ((), (), s32[]{:S(2)}) async-start(), calls=%async_computation.6 | async-start | bytes 42467328 | tf_op jit(solution)/shard_map/all_gather | solution.py:130
  687.0 1.4 copy-start.7
  711.2 66.1 %all-to-all-start.1 = ((bf16[4,16,14,1536]{3,1,2,0:T(8,128)(2,1)}), bf16[4,16,14,1536]{3,1,2,0:T(8,128)(2,1)S(1)}, u32[]{:S(2)}, u32[]{:S(2)}) async-start(bf16[4,16,14,1536]{3,1,2,0:T(8,128)(2,1)} %copy.84), calls=%async_computation.1 | async-start | bytes 5505024 | tf_op jit(solution)/shard_map/all_to_all | solution.py:48
  791.8 3.3 copy-start.1
  791.8 3.3 copy-start.3
Sparse Core Ops, SparseCore 0:
  15.8 341.6 all-gather.2
  444.0 225.6 reduce-scatter.1
  687.1 179.4 all-gather.4
where the time goes:
time: 907 us; the launch traced here: 900 us
  waiting for transfers between devices  657 us (72%)
  local copies, waits for them, and re-layouts  131 us (14%)
  matrix products  62.7 us (7%)
  other arithmetic  18.9 us (2%)
  starting transfers between devices  15.2 us (2%)
  between operations  14.4 us (2%)
    all_gather x1, waiting for transfers between devices, per_device(): full_pair = lax.all_gather(expert_pair, ('role', 'dp'), axis=2, tiled=True)  255 us
    reduce_scatter x1, waiting for transfers between devices, per_device(): lax.psum_scatter((total * (1.0 / math.sqrt(hidden_units))).reshape(lax.ax...  221 us
    all_gather x1, waiting for transfers between devices, per_device(): new_down = lax.all_gather(new_part, ('role', 'dp'), axis=1, tiled=True)  70.6 us
    all_to_all x1, waiting for transfers between devices, expert_pass(): lax.all_to_all(output.astype(jnp.bfloat16), 'ep', split_axis=0, concat_ax...  60.8 us
    all_to_all x1, waiting for transfers between devices, per_device(): lax.all_to_all(slot_latent, 'ep', split_axis=0, concat_axis=0, tiled=True)  50.5 us
    convert_element_type x1, local copies, waits for them, and re-layouts, per_device(): share = lax.psum_scatter((total * (1.0 / math.sqrt(hidden_units))).reshap...  48.6 us
    unnamed x20, local copies, waits for them, and re-layouts  43 us
    dot_general x1, matrix products, expert_pass(): jnp.einsum('jlch,lhd->jlcd', hidden, w_down, preferred_element_type=jnp.f...  19.8 us
  transfers between devices with their start and end apart: 6, of which 5 were waited for; matrix products, arithmetic and copies ran while one was open for 10% of the time, Pallas kernels for 0%

commit v1 on v0

--- a/solution.py
+++ b/solution.py
@@ -3,6 +3,8 @@
 import jax
 import jax.numpy as jnp
 from jax import lax
+from jax.experimental import pallas as pl
+from jax.experimental.pallas import tpu as pltpu
 from jax.sharding import PartitionSpec as P
 
 CAP = 7
@@ -51,7 +53,7 @@
     return (returned, hidden)
 
 
-def per_device(latents, noise, expert_ids, gate_values, advantages, expert_pair):
+def slot_plan(latents, noise, expert_ids, gate_values, advantages, expert_pair):
     ep_size = lax.axis_size("ep")
     group_size = lax.axis_size("role") * lax.axis_size("dp")
     local_experts = expert_pair.shape[0]
@@ -131,6 +133,141 @@
     return (current.reshape(image_count, tok_count, width), new_down)
 
 
+def hidden_kernel(x_ref, gate_ref, up_ref, down_ref, act_ref, vel_ref, *, units, in_scale, out_scale, chunk):
+    rows = x_ref.shape[0]
+    columns = chunk * units
+    total = up_ref.shape[0]
+    x = x_ref[...]
+    lane = lax.broadcasted_iota(jnp.int32, (rows, columns), 1)
+    for start in range(0, total, columns):
+        pre = lax.dot_general(
+            x, up_ref[start : start + columns], (((1,), (1,)), ((), ())),
+            preferred_element_type=jnp.float32,
+        ) * in_scale
+        hidden = jax.nn.gelu(pre, approximate=True).astype(jnp.bfloat16).astype(jnp.float32)
+        first = start // units
+        gate = jnp.broadcast_to(gate_ref[:, first : first + 1], (rows, columns))
+        for k in range(1, chunk):
+            gate = jnp.where(lane >= k * units, gate_ref[:, first + k : first + k + 1], gate)
+        act_ref[:, start : start + columns] = (hidden * gate).astype(jnp.bfloat16)
+    part = jnp.dot(act_ref[...], down_ref[...], preferred_element_type=jnp.float32) * out_scale
+    part = part.astype(jnp.bfloat16)
+    _, inner, _, tokens, _ = vel_ref.shape
+    cores = vel_ref.shape[0]
+    for j in range(inner):
+        for c in range(cores):
+            base = (j * cores + c) * tokens
+            vel_ref[c, j, 0] = part[base : base + tokens]
+
+
+def expert_chunk(experts, units):
+    chunk = 1
+    while chunk < experts and (chunk * units) % 128:
+        chunk *= 2
+    return chunk
+
+
+def token_plan(latents, noise, expert_ids, gate_values, advantages, expert_pair):
+    every = ("role", "ep", "dp")
+    roles = lax.axis_size("role")
+    eps = lax.axis_size("ep")
+    cores = lax.axis_size("dp")
+    devices = roles * eps * cores
+    local_experts, _, units, width = expert_pair.shape
+    image_count, tok_count, _ = latents.shape
+    tokens = image_count * tok_count
+    top_count = expert_ids.shape[3]
+    hidden_units = units * roles * cores
+    rows_all = tokens * devices
+    keep_gain, drift_gain, noise_gain = coefficients(0)
+    current = latents.reshape(tokens, width)
+    noise_now = noise[0].reshape(tokens, width)
+    factor = jnp.repeat(advantages * (drift_gain / noise_gain), tok_count)
+    scaled_noise = (factor[:, None] * noise_now.astype(jnp.float32)).astype(jnp.bfloat16)
+
+    picks = jnp.concatenate(
+        [
+            expert_ids[0].reshape(tokens, top_count).astype(jnp.float32).T,
+            gate_values[0].reshape(tokens, top_count).T,
+        ],
+        axis=0,
+    )
+    x_all = lax.all_gather(current, every, axis=0, tiled=True)
+    picks_all = lax.all_gather(picks, every, axis=0)
+    noise_all = lax.all_gather(scaled_noise, every, axis=0, tiled=True)
+    ids_all = picks_all[:, :top_count].astype(jnp.int32)
+    own = lax.axis_index("ep") * local_experts + jnp.arange(local_experts, dtype=jnp.int32)
+    match = ids_all[..., None] == own
+    gates = jnp.sum(jnp.where(match, picks_all[:, top_count:][..., None], 0.0), axis=1)
+    gates = gates.reshape(rows_all, local_experts)
+
+    w_up = expert_pair[:, 0].reshape(local_experts * units, width)
+    w_down = expert_pair[:, 1].reshape(local_experts * units, width)
+    inner = 2 if eps % 2 == 0 else 1
+    tile = inner * cores * tokens
+    steps_ep = eps // inner
+    chunk = expert_chunk(local_experts, units)
+    act, part = pl.pallas_call(
+        lambda *refs: hidden_kernel(
+            *refs, units=units, in_scale=1.0 / math.sqrt(width),
+            out_scale=1.0 / math.sqrt(hidden_units), chunk=chunk,
+        ),
+        grid=(rows_all // tile,),
+        in_specs=[
+            pl.BlockSpec((tile, width), lambda i: (i, 0)),
+            pl.BlockSpec((tile, local_experts), lambda i: (i, 0)),
+            pl.BlockSpec((local_experts * units, width), lambda i: (0, 0)),
+            pl.BlockSpec((local_experts * units, width), lambda i: (0, 0)),
+        ],
+        out_specs=[
+            pl.BlockSpec((tile, local_experts * units), lambda i: (i, 0)),
+            pl.BlockSpec(
+                (cores, inner, 1, tokens, width), lambda i: (0, i % steps_ep, i // steps_ep, 0, 0)
+            ),
+        ],
+        out_shape=[
+            jax.ShapeDtypeStruct((rows_all, local_experts * units), jnp.bfloat16),
+            jax.ShapeDtypeStruct((cores, eps, roles, tokens, width), jnp.bfloat16),
+        ],
+        compiler_params=pltpu.CompilerParams(
+            dimension_semantics=("arbitrary",), vmem_limit_bytes=56 * 1024 * 1024
+        ),
+        cost_estimate=pl.CostEstimate(
+            flops=4 * rows_all * width * local_experts * units,
+            bytes_accessed=6 * rows_all * width,
+            transcendentals=rows_all * local_experts * units,
+        ),
+        name="hidden_and_part",
+    )(x_all, gates, w_up, w_down)
+
+    rate = 10.0 / math.sqrt(tok_count * eps * top_count * image_count * roles * cores / (local_experts * eps))
+    total = lax.dot_general(act, noise_all, (((0,), (0,)), ((), ())), preferred_element_type=jnp.float32)
+    new_part = w_down.astype(jnp.float32) + (rate / math.sqrt(hidden_units)) * total
+    new_part = new_part.astype(jnp.bfloat16).reshape(local_experts, units, width)
+    new_down = lax.all_gather(new_part, ("role", "dp"), axis=1, tiled=True)
+
+    for name in ("dp", "ep", "role"):
+        swapped = lax.all_to_all(part, name, split_axis=0, concat_axis=0, tiled=True)
+        velocity = jnp.sum(swapped.astype(jnp.float32), axis=0)
+        part = velocity.astype(jnp.bfloat16)
+    moved = (
+        keep_gain * current.astype(jnp.float32)
+        + drift_gain * velocity
+        + noise_gain * noise_now.astype(jnp.float32)
+    )
+    return (moved.astype(jnp.bfloat16).reshape(latents.shape), new_down)
+
+
+def per_device(latents, noise, expert_ids, gate_values, advantages, expert_pair):
+    devices = lax.axis_size(("role", "ep", "dp"))
+    groups = lax.axis_size(("role", "dp"))
+    images = latents.shape[0] * groups
+    all_tokens = latents.shape[0] * latents.shape[1] * devices
+    slots = expert_pair.shape[0] * images * lax.axis_size("ep") * CAP
+    plan = token_plan if all_tokens <= slots else slot_plan
+    return plan(latents, noise, expert_ids, gate_values, advantages, expert_pair)
+
+
 def solution(mesh):
     in_specs = (
         P(("role", "dp"), "ep", None),

time: 907 us -> 477 us (0.53)
  waiting for transfers between devices: 657 us -> 80 us
  blocking collectives: 0 us -> 239 us
  local copies, waits for them, and re-layouts: 131 us -> 36.8 us
  Pallas kernels: 0 us -> 58.8 us
  matrix products: 62.7 us -> 27.5 us
  starting transfers between devices: 15.2 us -> 0.12 us
    all_gather x2 -> x3, waiting for transfers between devices: 325 us -> 79.3 us  [the longest x1 40.7 us: token_plan(): x_all = lax.all_gather(current, every, axis=0, tiled=True)]
    reduce_scatter x1 -> x0, waiting for transfers between devices: 221 us -> none  [per_device(): lax.psum_scatter((total * (1.0 / math.sqrt(hidden_units))).reshape(lax.ax...]
    all_to_all x0 -> x3, blocking collectives: none -> 193 us  [token_plan(): lax.all_to_all(part, name, split_axis=0, concat_axis=0, tiled=True)]
    all_to_all x3 -> x0, waiting for transfers between devices: 111 us -> none  [the longest x1 60.8 us: expert_pass(): lax.all_to_all(output.astype(jnp.bfloat16), 'ep', split_axis=0, concat_ax...]
    pallas_call x0 -> x1, Pallas kernels: none -> 58.8 us  [token_plan(): pl.pallas_call(lambda *refs: hidden_kernel(*refs, units=units, in_scale=1...]
    convert_element_type x2 -> x1, local copies, waits for them, and re-layouts: 51.7 us -> 0.08 us  [token_plan(): expert_ids[0].reshape(tokens, top_count).astype(jnp.float32)]
    all_gather x0 -> x1, blocking collectives: none -> 45.8 us  [token_plan(): picks_all = lax.all_gather(picks, every, axis=0)]
    dot_general x5 -> x1, matrix products: 62.7 us -> 27.5 us  [token_plan(): lax.dot_general(act, noise_all, (((0,), (0,)), ((), ())), preferred_eleme...]
  transfers between devices with their start and end apart: 6 -> 3, of which waited for: 5 -> 2; matrix products, arithmetic and copies ran while one was open for 10% -> 7% of each run, Pallas kernels for 0% -> 12%
where the time goes in v1:
time: 477 us; the launch traced here: 476 us
  blocking collectives  239 us (50%)
  waiting for transfers between devices  80 us (17%)
  Pallas kernels  58.8 us (12%)
  local copies, waits for them, and re-layouts  36.8 us (8%)
  matrix products  27.5 us (6%)
  other arithmetic  20.3 us (4%)
  between operations  13.8 us (3%)
    all_to_all x3, blocking collectives, token_plan(): lax.all_to_all(part, name, split_axis=0, concat_axis=0, tiled=True)  193 us
    pallas_call x1, Pallas kernels, token_plan(): pl.pallas_call(lambda *refs: hidden_kernel(*refs, units=units, in_scale=1...  58.8 us
    all_gather x1, blocking collectives, token_plan(): picks_all = lax.all_gather(picks, every, axis=0)  45.8 us
    all_gather x1, waiting for transfers between devices, token_plan(): x_all = lax.all_gather(current, every, axis=0, tiled=True)  40.7 us
    all_gather x1, waiting for transfers between devices, token_plan(): noise_all = lax.all_gather(scaled_noise, every, axis=0, tiled=True)  38.6 us
    dot_general x1, matrix products, token_plan(): lax.dot_general(act, noise_all, (((0,), (0,)), ((), ())), preferred_eleme...  27.5 us
    unnamed x5, local copies, waits for them, and re-layouts  25.4 us
    reduce_sum x3, other arithmetic, token_plan(): velocity = jnp.sum(swapped.astype(jnp.float32), axis=0)  15.8 us
  transfers between devices with their start and end apart: 3, of which 2 were waited for; matrix products, arithmetic and copies ran while one was open for 7% of the time, Pallas kernels for 12%

profile of v1, /device:TPU:0, one launch (start us, length us, event | category | flops | bytes accessed | tf_op | source)
XLA Modules:
  0.0 476.3 jit_solution(111941931001127041)
XLA Ops:
  7.2 0.0 all-gather.6.cloned.1.call-start
  7.2 0.7 all-gather.6.cloned.1.call-update
  7.9 0.0 all-gather.8.cloned.1.call-start
  7.9 0.7 broadcast_multiply_fusion.1
  8.6 0.1 broadcast_in_dim.20
  8.7 0.1 mul.59
  8.8 1.9 fusion.2
  10.6 0.0 all-gather.8.cloned.1.call-update
  10.7 0.0 all-gather.10.cloned.1.call-start
  10.7 0.8 reshape_squeeze.11
  11.5 0.7 convert_element_type.45
  12.2 0.1 convert_element_type.46
  12.3 45.8 %all-gather.1 = f32[32,12,128]{2,1,0:T(8,128)S(1)} all-gather(f32[1,12,128]{2,1,0:T(8,128)S(1)} %maximum_bitcast_fusion), channel_id=2, replica_groups=mesh['role'=4,'ep'=4,'dp'=2] {'role','ep','dp'}, dimensions={0}, use_global_device_ids=true | all-gather | bytes 202752 | tf_op jit(solution)/shard_map/all_gather | solution.py:196
  58.1 0.2 select_reduce_fusion
  58.4 1.9 copy.8
  60.3 8.5 %fusion.4 = (bf16[16,1,96,1536]{3,2,1,0:T(8,128)(2,1)}, bf16[16,1,96,1536]{3,2,1,0:T(8,128)(2,1)}) fusion(bf16[16,2,96,1536]{3,2,1,0:T(8,128)(2,1)} %param.11), kind=kLoop, calls=%fused_computation.14 | loop fusion | bytes 18874368 | tf_op jit(solution)/shard_map/slice | solution.py:205
  68.7 40.7 %all-gather.6.cloned.1.call-done.refs_0_ = bf16[4096,1536]{1,0:T(8,128)(2,1)} async-done(((bf16[128,1536]{1,0:T(8,128)(2,1)}), bf16[4096,1536]{1,0:T(8,128)(2,1)}) %all-gather.6.cloned.1.call-update) | async-done | bytes 12582928 | tf_op jit(solution)/shard_map/all_gather | solution.py:195
  109.5 58.8 %hidden_and_part.1 = (bf16[4096,1536]{1,0:T(8,128)(2,1)}, bf16[2,4,4,128,1536]{4,3,2,1,0:T(8,128)(2,1)}) custom-call(bf16[4096,1536]{1,0:T(8,128)(2,1)} %all-gather.6.cloned.1.call-done.refs_0_, f32[4096,16]{1,0:T(8,128)} %bitcast.29, bf16[1536,1536]{1,0:T(8,128)(2,1)} %bitcast.27, bf16[1536,1536]{1,0:T(8,128)(2,1)} %bitcast.25), custom_call_target="tpu_custom_call" | custom-call | flops 38654705664 | bytes 37748736 | tf_op jit(solution)/shard_map/hidden_and_part/pallas_call | solution.py:210
  168.3 38.6 %all-gather.8.cloned.1.call-done = bf16[4096,1536]{1,0:T(8,128)(2,1)} async-done(((bf16[128,1536]{1,0:T(8,128)(2,1)}), bf16[4096,1536]{1,0:T(8,128)(2,1)}) %all-gather.8.cloned.1.call-update) | async-done | bytes 12582928 | tf_op jit(solution)/shard_map/all_gather | solution.py:197
  206.9 27.5 %fusion.1 = bf16[1536,1536]{1,0:T(8,128)(2,1)} fusion(bf16[4096,1536]{1,0:T(8,128)(2,1)} %get-tuple-element.5, bf16[4096,1536]{1,0:T(8,128)(2,1)} %all-gather.8.cloned.1.call-done, bf16[1536,1536]{1,0:T(8,128)(2,1)} %bitcast.26), kind=kOutput, calls=%fused_computation.2 | convolution fusion | flops 19336790016 | bytes 34603008 | tf_op jit(solution)/shard_map/dot_general | solution.py:244
  234.4 0.0 all-gather.10.cloned.1.call-update
  234.5 25.6 %all_to_all.15 = bf16[2,4,4,128,1536]{4,3,2,1,0:T(8,128)(2,1)} all-to-all(bf16[2,4,4,128,1536]{4,3,2,1,0:T(8,128)(2,1)} %get-tuple-element.4), channel_id=1, replica_groups=mesh['role'=4,'ep'=4,'dp'=2] {'dp'}, dimensions={0} | all-to-all | bytes 25165824 | tf_op jit(solution)/shard_map/all_to_all | solution.py:250
  260.1 11.5 %reduce_sum.43 = bf16[4,4,128,1536]{3,2,1,0:T(8,128)(2,1)} reduce(bf16[2,4,4,128,1536]{4,3,2,1,0:T(8,128)(2,1)} %all_to_all.15, bf16[]{:T(256)} %constant.18.clone.1), dimensions={0}, to_apply=%region_1.2 | reduce | flops 3145728 | bytes 18874370 | tf_op jit(solution)/shard_map/reduce_sum | solution.py:251
  271.6 145.4 %all_to_all.16 = bf16[4,4,128,1536]{3,2,1,0:T(8,128)(2,1)} all-to-all(bf16[4,4,128,1536]{3,2,1,0:T(8,128)(2,1)} %reduce_sum.43), channel_id=1, replica_groups=mesh['role'=4,'ep'=4,'dp'=2] {'ep'}, dimensions={0} | all-to-all | bytes 12582912 | tf_op jit(solution)/shard_map/all_to_all | solution.py:250
  417.1 4.1 reduce_sum.44
  421.2 22.0 %all_to_all.17 = bf16[4,128,1536]{2,1,0:T(8,128)(2,1)S(1)} all-to-all(bf16[4,128,1536]{2,1,0:T(8,128)(2,1)S(1)} %reduce_sum.44), channel_id=1, replica_groups=mesh['role'=4,'ep'=4,'dp'=2] {'role'}, dimensions={0} | all-to-all | bytes 3145728 | tf_op jit(solution)/shard_map/all_to_all | solution.py:250
  443.1 0.2 convert_reduce_fusion
  443.4 0.1 broadcast_multiply_fusion
  443.4 0.0 copy-done
  443.5 0.0 copy-done.1
  443.5 0.9 fusion.3
  444.4 25.4 %copy.10 = bf16[16,768,1536]{2,1,0:T(8,128)(2,1)} copy(bf16[16,768,1536]{2,1,0:T(8,128)(2,1)} %all-gather.10.cloned.1.call-done) | data formatting | bytes 75497472
  (6 shorter events, 0.0 us)
Async XLA Ops:
  7.2 102.3 %all-gather.6.cloned.1.call-start = ((), (), s32[]{:S(2)}) async-start(), calls=%async_computation.3 | async-start | bytes 12976128 | tf_op jit(solution)/shard_map/all_gather | solution.py:195
  7.9 199.0 %all-gather.8.cloned.1.call-start = ((), (), s32[]{:S(2)}) async-start(), calls=%async_computation.4 | async-start | bytes 12976128 | tf_op jit(solution)/shard_map/all_gather | solution.py:197
  10.7 433.7 %all-gather.10.cloned.1.call-start = ((), (), s32[]{:S(2)}) async-start(), calls=%async_computation.5 | async-start | bytes 42467328 | tf_op jit(solution)/shard_map/all_gather | solution.py:247
  417.1 26.4 %copy-start = (bf16[2,64,1536]{2,1,0:T(8,128)(2,1)S(1)}, bf16[2,64,1536]{2,1,0:T(8,128)(2,1)}, u32[]{:S(2)}) copy-start(bf16[2,64,1536]{2,1,0:T(8,128)(2,1)} %param.6) | copy-start | bytes 1179652
  417.1 26.4 %copy-start.1 = (bf16[1,2,64,1536]{3,2,1,0:T(8,128)(2,1)S(1)}, bf16[1,2,64,1536]{3,2,1,0:T(8,128)(2,1)}, u32[]{:S(2)}) copy-start(bf16[1,2,64,1536]{3,2,1,0:T(8,128)(2,1)} %param.7) | copy-start | bytes 1179652
Sparse Core Ops, SparseCore 0:
  11.0 98.4 all-gather.5
  113.1 93.8 all-gather.7
  234.6 177.9 all-gather.9

commit v2 on v0

--- a/solution.py
+++ b/solution.py
@@ -3,9 +3,13 @@
 import jax
 import jax.numpy as jnp
 from jax import lax
+from jax.experimental import pallas as pl
+from jax.experimental.pallas import tpu as pltpu
 from jax.sharding import PartitionSpec as P
 
+
 CAP = 7
+VMEM_BYTES = 56 * 1024 * 1024
 
 
 def coefficients(section):
@@ -51,7 +55,7 @@
     return (returned, hidden)
 
 
-def per_device(latents, noise, expert_ids, gate_values, advantages, expert_pair):
+def slot_plan(latents, noise, expert_ids, gate_values, advantages, expert_pair):
     ep_size = lax.axis_size("ep")
     group_size = lax.axis_size("role") * lax.axis_size("dp")
     local_experts = expert_pair.shape[0]
@@ -131,6 +135,406 @@
     return (current.reshape(image_count, tok_count, width), new_down)
 
 
+def swap(x, axis, bit):
+    return lax.ppermute(x, axis, [(i, i ^ bit) for i in range(lax.axis_size(axis))])
+
+
+def from_ahead(x, step):
+    size = lax.axis_size("ep")
+    return lax.ppermute(x, "ep", [((i + step) % size, i) for i in range(size)])
+
+
+def to_ahead(x, step):
+    size = lax.axis_size("ep")
+    return lax.ppermute(x, "ep", [(i, (i + step) % size) for i in range(size)])
+
+
+def plane_neighbours(block):
+    return swap(block, "role", 1), swap(block, "role", 2)
+
+
+def plane_diagonal(first, second):
+    half = first.shape[0] // 2
+    return swap(first[:half], "role", 2), swap(second[half:], "role", 1)
+
+
+def spread_along(rows):
+    return [from_ahead(rows, step) for step in range(1, lax.axis_size("ep"))]
+
+
+def near_layout(count):
+    half = count // 2
+    copies = [(n, 0, count, n * count) for n in range(3)]
+    return copies + [(3, 0, half, 3 * count), (4, 0, half, 3 * count + half)]
+
+
+def far_layout(count, steps):
+    copies = []
+    half = steps * count // 2
+    for s in range(steps):
+        low, high = s * count, (s + 1) * count
+        base = 4 * low
+        copies += [(n, low, count, base + n * count) for n in range(3)]
+        if low < half:
+            copies.append((3, low, min(high, half) - low, base + 3 * count))
+        if high > half:
+            start = max(low, half)
+            copies.append((4, start - half, high - start, base + 3 * count + start - low))
+    return copies
+
+
+def piece_copies(pieces, target, sems, layout, offset=0):
+    return [
+        pltpu.make_async_copy(
+            pieces[n].at[pl.ds(first, size)], target.at[pl.ds(offset + start, size)], sems.at[k]
+        )
+        for k, (n, first, size, start) in enumerate(layout)
+    ]
+
+
+def hidden_kernel(*refs, layout, width, columns, in_scale, out_scale):
+    pieces = refs[:-7]
+    up_ref, down_ref, pick_ref, act_ref, part_ref, x_ref, sems = refs[-7:]
+    tile = act_ref.shape[0]
+    step = pl.program_id(0)
+    copies = piece_copies(pieces, x_ref, sems, layout)
+
+    @pl.when(step == 0)
+    def _():
+        for copy in copies:
+            copy.start()
+
+    for k in range(x_ref.shape[0] // tile):
+
+        @pl.when(step == k)
+        def _(k=k):
+            for copy, entry in zip(copies, layout):
+                if entry[3] // tile == k:
+                    copy.wait()
+
+    rows = pl.ds(pl.multiple_of(step * tile, tile), tile)
+    x = x_ref[rows, :width]
+    gates = x_ref[rows, width:]
+    for start in range(0, up_ref.shape[0], columns):
+        pre = lax.dot_general(
+            x, up_ref[start : start + columns], (((1,), (1,)), ((), ())),
+            preferred_element_type=jnp.float32,
+        ) * in_scale
+        hidden = jax.nn.gelu(pre, approximate=True).astype(jnp.bfloat16).astype(jnp.float32)
+        gate = jnp.dot(gates, pick_ref[:, start : start + columns], preferred_element_type=jnp.float32)
+        act_ref[:, start : start + columns] = (hidden * gate).astype(jnp.bfloat16)
+    part = jnp.dot(act_ref[...], down_ref[...], preferred_element_type=jnp.float32) * out_scale
+    part_ref[...] = part.astype(jnp.bfloat16)
+
+
+def column_span(total):
+    for parts in (4, 3, 2):
+        if total % (parts * 128) == 0:
+            return total // parts
+    return total
+
+
+def hidden_and_part(pieces, layout, gate_width, w_up, w_down, pick, hidden_units, tile):
+    total, width = w_up.shape
+    count = sum(entry[2] for entry in layout)
+    return pl.pallas_call(
+        lambda *refs: hidden_kernel(
+            *refs, layout=layout, width=width, columns=column_span(total),
+            in_scale=1.0 / math.sqrt(width), out_scale=1.0 / math.sqrt(hidden_units),
+        ),
+        grid=(count // tile,),
+        in_specs=[pl.BlockSpec(memory_space=pl.ANY)] * len(pieces)
+        + [
+            pl.BlockSpec((total, width), lambda i: (0, 0)),
+            pl.BlockSpec((total, width), lambda i: (0, 0)),
+            pl.BlockSpec((gate_width, total), lambda i: (0, 0)),
+        ],
+        out_specs=[
+            pl.BlockSpec((tile, total), lambda i: (i, 0)),
+            pl.BlockSpec((tile, width), lambda i: (i, 0)),
+        ],
+        out_shape=[
+            jax.ShapeDtypeStruct((count, total), jnp.bfloat16),
+            jax.ShapeDtypeStruct((count, width), jnp.bfloat16),
+        ],
+        scratch_shapes=[
+            pltpu.VMEM((count, width + gate_width), jnp.bfloat16),
+            pltpu.SemaphoreType.DMA((len(layout),)),
+        ],
+        compiler_params=pltpu.CompilerParams(
+            dimension_semantics=("arbitrary",), vmem_limit_bytes=VMEM_BYTES
+        ),
+        cost_estimate=pl.CostEstimate(
+            flops=4 * count * width * total,
+            bytes_accessed=6 * count * width + 4 * total * width,
+            transcendentals=count * total,
+        ),
+        name="hidden_and_part",
+    )(*pieces, w_up, w_down, pick)
+
+
+def update_kernel(*refs, layouts, scale):
+    groups = len(layouts)
+    pieces = refs[: 5 * groups]
+    acts = refs[5 * groups : 6 * groups]
+    down_ref, out_ref, noise_ref, sems = refs[6 * groups :]
+    counts = [sum(entry[2] for entry in layout) for layout in layouts]
+    offsets = [sum(counts[:g]) for g in range(groups)]
+
+    @pl.when(pl.program_id(0) == 0)
+    def _():
+        copies = []
+        for g in range(groups):
+            copies += piece_copies(
+                pieces[5 * g : 5 * g + 5], noise_ref, sems.at[g], layouts[g], offsets[g]
+            )
+        for copy in copies:
+            copy.start()
+        for copy in copies:
+            copy.wait()
+
+    total = jnp.zeros(out_ref.shape, jnp.float32)
+    for g in range(groups):
+        total = total + lax.dot_general(
+            acts[g][...], noise_ref[offsets[g] : offsets[g] + counts[g]], (((0,), (0,)), ((), ())),
+            preferred_element_type=jnp.float32,
+        )
+    out_ref[...] = (down_ref[...].astype(jnp.float32) + scale * total).astype(jnp.bfloat16)
+
+
+def updated_rows(pieces, layouts, acts, w_down, scale, columns, first, steps):
+    counts = [sum(entry[2] for entry in layout) for layout in layouts]
+    rows = sum(counts)
+    width = w_down.shape[1]
+    flat = [piece for group in pieces for piece in group]
+    return pl.pallas_call(
+        lambda *refs: update_kernel(*refs, layouts=layouts, scale=scale),
+        grid=(steps,),
+        in_specs=[pl.BlockSpec(memory_space=pl.ANY)] * len(flat)
+        + [
+            pl.BlockSpec((count, columns), lambda i, block=block: (block, first + i))
+            for count, (_, block) in zip(counts, acts)
+        ]
+        + [pl.BlockSpec((columns, width), lambda i: (first + i, 0))],
+        out_specs=pl.BlockSpec((columns, width), lambda i: (i, 0)),
+        out_shape=jax.ShapeDtypeStruct((steps * columns, width), jnp.bfloat16),
+        scratch_shapes=[
+            pltpu.VMEM((rows, width), jnp.bfloat16),
+            pltpu.SemaphoreType.DMA((len(layouts), max(len(layout) for layout in layouts))),
+        ],
+        compiler_params=pltpu.CompilerParams(
+            dimension_semantics=("arbitrary",), vmem_limit_bytes=VMEM_BYTES
+        ),
+        cost_estimate=pl.CostEstimate(
+            flops=2 * rows * width * columns * steps,
+            bytes_accessed=2 * rows * width + 8 * columns * steps * width,
+            transcendentals=0,
+        ),
+        name="updated_rows",
+    )(*flat, *[act for act, _ in acts], w_down)
+
+
+def place_kernel(*refs, first, starts, cores):
+    pieces = refs[: len(starts)]
+    out, held, in_sems, out_sems = refs[-4:]
+    role = lax.axis_index("role")
+    core = lax.axis_index("dp")
+    loads, stores = [], []
+    row = 0
+    for n, (offset, role_bit, core_bit) in enumerate(starts):
+        slot = (role ^ role_bit) * cores + (core ^ core_bit)
+        size = pieces[n].shape[0]
+        room = held.at[pl.ds(row, size)]
+        loads.append(pltpu.make_async_copy(pieces[n], room, in_sems.at[n]))
+        stores.append(
+            pltpu.make_async_copy(room, out.at[pl.ds(first + offset, size), slot], out_sems.at[n])
+        )
+        row += size
+    for load in loads:
+        load.start()
+    for load, store in zip(loads, stores):
+        load.wait()
+        store.start()
+    for store in stores:
+        store.wait()
+
+
+def place(out, pieces, first, starts, shape, cores):
+    operands = list(pieces) + ([] if out is None else [out])
+    rows = sum(piece.shape[0] for piece in pieces)
+    return pl.pallas_call(
+        lambda *refs: place_kernel(*refs, first=first, starts=starts, cores=cores),
+        in_specs=[pl.BlockSpec(memory_space=pl.ANY)] * len(operands),
+        out_specs=pl.BlockSpec(memory_space=pl.ANY),
+        out_shape=jax.ShapeDtypeStruct(shape, jnp.bfloat16),
+        scratch_shapes=[
+            pltpu.VMEM((rows,) + shape[2:], jnp.bfloat16),
+            pltpu.SemaphoreType.DMA((len(pieces),)),
+            pltpu.SemaphoreType.DMA((len(pieces),)),
+        ],
+        input_output_aliases={} if out is None else {len(pieces): 0},
+        compiler_params=pltpu.CompilerParams(vmem_limit_bytes=VMEM_BYTES),
+        name="place",
+    )(*operands)
+
+
+def other_core(pieces):
+    return [swap(piece, "dp", 1) for piece in pieces]
+
+
+def token_plan(latents, noise, expert_ids, gate_values, advantages, expert_pair):
+    roles = lax.axis_size("role")
+    eps = lax.axis_size("ep")
+    cores = lax.axis_size("dp")
+    local_experts, _, units, width = expert_pair.shape
+    experts = local_experts * eps
+    image_count, tok_count, _ = latents.shape
+    tokens = image_count * tok_count
+    top_count = expert_ids.shape[3]
+    hidden_units = units * roles * cores
+    gate_width = 2 * experts
+    keep_gain, drift_gain, noise_gain = coefficients(0)
+    current = latents.reshape(tokens, width)
+    noise_now = noise[0].reshape(tokens, width)
+    factor = jnp.repeat(advantages * (drift_gain / noise_gain), tok_count)
+    scaled_noise = (factor[:, None] * noise_now.astype(jnp.float32)).astype(jnp.bfloat16)
+
+    ids = expert_ids[0].reshape(tokens, top_count)
+    values = gate_values[0].reshape(tokens, top_count)
+    match = ids[..., None] == jnp.arange(experts, dtype=jnp.int32)
+    table = jnp.sum(jnp.where(match, values[..., None], 0.0), axis=1)
+    table_high = lax.reduce_precision(table, 8, 7)
+    table_low = table - table_high
+    rows = jnp.concatenate(
+        [current, table_high.astype(jnp.bfloat16), table_low.astype(jnp.bfloat16)], axis=1
+    )
+    own = lax.axis_index("ep") * local_experts + jnp.arange(local_experts * units, dtype=jnp.int32) // units
+    source = jnp.arange(gate_width, dtype=jnp.int32) % experts
+    pick = (source[:, None] == own[None, :]).astype(jnp.bfloat16)
+    w_up = expert_pair[:, 0].reshape(local_experts * units, width)
+    w_down = expert_pair[:, 1].reshape(local_experts * units, width)
+    tile = roles * tokens
+    close = near_layout(tokens)
+    distant = far_layout(tokens, eps - 1)
+
+    def hidden(pieces, layout):
+        return hidden_and_part(pieces, layout, gate_width, w_up, w_down, pick, hidden_units, tile)
+
+    row_along = spread_along(rows)
+    row_near = [rows, *plane_neighbours(rows)]
+    row_near += plane_diagonal(*row_near[1:])
+    row_near_there = other_core(row_near)
+    scaled_noise, row_along = lax.optimization_barrier((scaled_noise, row_along))
+    noise_along = spread_along(scaled_noise)
+    row_stack = jnp.concatenate(row_along, axis=0)
+    row_far = [row_stack, *plane_neighbours(row_stack)]
+    row_far += plane_diagonal(*row_far[1:])
+    row_far_there = other_core(row_far)
+    both = close + [(5 + n, first, size, tile + start) for n, first, size, start in close]
+    act_near, part_near = hidden(row_near + row_near_there, both)
+
+    noise_stack = jnp.concatenate(noise_along, axis=0)
+    held = lax.optimization_barrier((scaled_noise, noise_stack, row_far[1], row_far[2]))
+    noise_far = [held[1], *plane_neighbours(held[1])]
+    noise_near = [held[0], *plane_neighbours(held[0])]
+    act_far_here, part_far_here = hidden(row_far, distant)
+    noise_far += plane_diagonal(*noise_far[1:])
+    noise_near += plane_diagonal(*noise_near[1:])
+    near_early = other_core(noise_near[:3])
+    far_early = other_core(noise_far[:3])
+    act_far_there, part_far_there = hidden(row_far_there, distant)
+    noise_near_there = near_early + other_core(noise_near[3:])
+    noise_far_there = far_early + other_core(noise_far[3:])
+
+    line = part_near[:tile].astype(jnp.float32)
+    line = line + swap(part_near[tile:], "dp", 1).astype(jnp.float32)
+    pair = part_far_here.astype(jnp.float32) + swap(part_far_there, "dp", 1).astype(jnp.float32)
+    pair = pair.astype(jnp.bfloat16).reshape(eps - 1, roles * tokens, width)
+    back = [to_ahead(pair[step - 1], step) for step in range(1, eps)]
+    for piece in back:
+        line = line + piece.astype(jnp.float32)
+    line = line.reshape(roles, tokens, width)
+    velocity = line[0]
+    for bit in range(1, roles):
+        velocity = velocity + swap(line[bit].astype(jnp.bfloat16), "role", bit).astype(jnp.float32)
+    moved = (
+        keep_gain * current.astype(jnp.float32)
+        + drift_gain * velocity
+        + noise_gain * noise_now.astype(jnp.float32)
+    )
+
+    rate = 10.0 / math.sqrt(tok_count * eps * top_count * image_count * roles * cores / experts)
+    step_scale = rate / math.sqrt(hidden_units)
+    shape = (local_experts, roles * cores, units, width)
+    chunks = 4
+    chunk = local_experts // chunks
+    columns = chunk * units
+    acts = ((act_near, 0), (act_far_here, 0), (act_near, 1), (act_far_there, 0))
+    noises = (noise_near, noise_far, noise_near_there, noise_far_there)
+    layouts = (close, distant, close, distant)
+    head = updated_rows(noises, layouts, acts, w_down, step_scale, columns, 0, 1)
+    rest = updated_rows(noises, layouts, acts, w_down, step_scale, columns, 1, chunks - 1)
+    new_down = None
+    waiting = []
+    sent = []
+    starts = [(0, 0, 0), (0, 1, 0), (0, 2, 0), (0, 3, 0), (chunk // 2, 3, 0)]
+    starts += [(offset, bit, 1) for offset, bit, _ in starts]
+    for c in range(chunks):
+        last = c == chunks - 1
+        mine = head if c == 0 else rest[(c - 1) * columns : c * columns]
+        mine = mine.reshape(chunk, units, width)
+
+        def place_next(value):
+            nonlocal new_down
+            n, pieces = waiting.pop(0)
+            new_down = place(new_down, pieces, n * chunk, starts, shape, cores)
+            value, new_down = lax.optimization_barrier((value, new_down))
+            return value
+
+        if len(sent) >= 2:
+            mine, _ = lax.optimization_barrier((mine, sent[-2]))
+        near = plane_neighbours(mine)
+        sent.append(near)
+        early = other_core([mine, *near])
+        if last:
+            near = place_next(near)
+        diagonal = plane_diagonal(*near)
+        if last:
+            diagonal = place_next(diagonal)
+        late = other_core(diagonal)
+        if last:
+            late = place_next(late)
+        waiting.append((c, [mine, *near, *diagonal, *early, *late]))
+    n, pieces = waiting.pop(0)
+    new_down = place(new_down, pieces, n * chunk, starts, shape, cores)
+    new_down = new_down.reshape(local_experts, hidden_units, width)
+    return (moved.astype(jnp.bfloat16).reshape(latents.shape), new_down)
+
+
+def per_device(latents, noise, expert_ids, gate_values, advantages, expert_pair):
+    devices = lax.axis_size(("role", "ep", "dp"))
+    groups = lax.axis_size(("role", "dp"))
+    local_experts, _, units, width = expert_pair.shape
+    experts = local_experts * lax.axis_size("ep")
+    images = latents.shape[0] * groups
+    all_tokens = latents.shape[0] * latents.shape[1] * devices
+    slots = experts * images * CAP
+    fits = (
+        all_tokens <= slots
+        and lax.axis_size("role") == 4
+        and lax.axis_size("dp") == 2
+        and local_experts % 8 == 0
+        and (local_experts // 4 * units) % 128 == 0
+        and (latents.shape[0] * latents.shape[1]) % 32 == 0
+        and (2 * experts) % 128 == 0
+        and width % (2 * experts) == 0
+        and (local_experts * units) % 128 == 0
+    )
+    if not fits:
+        return slot_plan(latents, noise, expert_ids, gate_values, advantages, expert_pair)
+    return token_plan(latents, noise, expert_ids, gate_values, advantages, expert_pair)
+
+
 def solution(mesh):
     in_specs = (
         P(("role", "dp"), "ep", None),

time: 907 us -> 598 us (0.66)
  waiting for transfers between devices: 657 us -> 340 us
  Pallas kernels: 0 us -> 141 us
  local copies, waits for them, and re-layouts: 131 us -> 37.2 us
  matrix products: 62.7 us -> 0 us
  starting transfers between devices: 15.2 us -> 66.6 us
  between operations: 14.4 us -> 1.52 us
    ppermute x0 -> x86, waiting for transfers between devices: none -> 340 us  [the longest x77 185 us: swap(): lax.ppermute(x, axis, [(i, i ^ bit) for i in range(lax.axis_size(axis))])]
    all_gather x2 -> x0, waiting for transfers between devices: 325 us -> none  [the longest x1 255 us: per_device(): full_pair = lax.all_gather(expert_pair, ('role', 'dp'), axis=2, tiled=True)]
    reduce_scatter x1 -> x0, waiting for transfers between devices: 221 us -> none  [per_device(): lax.psum_scatter((total * (1.0 / math.sqrt(hidden_units))).reshape(lax.ax...]
    pallas_call x0 -> x9, Pallas kernels: none -> 141 us  [the longest x3 75.4 us: hidden_and_part(): pl.pallas_call(lambda *refs: hidden_kernel(*refs, layout=layout, width=wi...]
    all_to_all x3 -> x0, waiting for transfers between devices: 111 us -> none  [the longest x1 60.8 us: expert_pass(): lax.all_to_all(output.astype(jnp.bfloat16), 'ep', split_axis=0, concat_ax...]
    ppermute x0 -> x86, starting transfers between devices: none -> 66.6 us  [the longest x77 50.5 us: swap(): lax.ppermute(x, axis, [(i, i ^ bit) for i in range(lax.axis_size(axis))])]
    dot_general x5 -> x0, matrix products: 62.7 us -> none  [the longest x1 19.8 us: expert_pass(): jnp.einsum('jlch,lhd->jlcd', hidden, w_down, preferred_element_type=jnp.f...]
    convert_element_type x2 -> x0, local copies, waits for them, and re-layouts: 51.7 us -> none  [the longest x1 48.6 us: per_device(): share = lax.psum_scatter((total * (1.0 / math.sqrt(hidden_units))).reshap...]
  transfers between devices with their start and end apart: 6 -> 86, of which waited for: 5 -> 26; matrix products, arithmetic and copies ran while one was open for 10% -> 6% of each run, Pallas kernels for 0% -> 21%
where the time goes in v2:
time: 598 us
  waiting for transfers between devices  340 us (57%)
  Pallas kernels  141 us (24%)
  starting transfers between devices  66.6 us (11%)
  local copies, waits for them, and re-layouts  37.2 us (6%)
  other arithmetic  11.3 us (2%)
    ppermute x77, waiting for transfers between devices, swap(): lax.ppermute(x, axis, [(i, i ^ bit) for i in range(lax.axis_size(axis))])  185 us
    ppermute x3, waiting for transfers between devices, to_ahead(): return lax.ppermute(x, 'ep', [(i, (i + step) % size) for i in range(size)])  113 us
    pallas_call x3, Pallas kernels, hidden_and_part(): pl.pallas_call(lambda *refs: hidden_kernel(*refs, layout=layout, width=wi...  75.4 us
    ppermute x77, starting transfers between devices, swap(): lax.ppermute(x, axis, [(i, i ^ bit) for i in range(lax.axis_size(axis))])  50.5 us
    ppermute x6, waiting for transfers between devices, from_ahead(): return lax.ppermute(x, 'ep', [((i + step) % size, i) for i in range(size)])  41.4 us
    pallas_call x2, Pallas kernels, updated_rows(): pl.pallas_call(lambda *refs: update_kernel(*refs, layouts=layouts, scale=...  37.5 us
    pallas_call x4, Pallas kernels, place(): pl.pallas_call(lambda *refs: place_kernel(*refs, first=first, starts=star...  28.6 us
    slice x16, local copies, waits for them, and re-layouts, plane_diagonal(): return (swap(first[:half], 'role', 2), swap(second[half:], 'role', 1))  13 us
  transfers between devices with their start and end apart: 86, of which 26 were waited for; matrix products, arithmetic and copies ran while one was open for 6% of the time, Pallas kernels for 21%

profile of v2, /device:TPU:0, one launch (start us, length us, event | category | flops | bytes accessed | tf_op | source)
XLA Modules:
  0.0 597.7 jit_solution(13893278174128941415)
XLA Ops:
  3.6 5.1 collective-permute-start.10
  11.4 7.5 %collective-permute-done.10 = bf16[128,1664]{1,0:T(8,128)(2,1)S(1)} collective-permute-done((bf16[128,1664]{1,0:T(8,128)(2,1)S(1)}, bf16[128,1664]{1,0:T(8,128)(2,1)S(1)}, u32[]{:S(2)}, u32[]{:S(2)}) %collective-permute-start.10) | collective-permute-done | bytes 426016 | tf_op jit(solution)/shard_map/ppermute | solution.py:144
  19.0 26.1 %collective-permute-done.11 = bf16[128,1664]{1,0:T(8,128)(2,1)S(1)} collective-permute-done((bf16[128,1664]{1,0:T(8,128)(2,1)S(1)}, bf16[128,1664]{1,0:T(8,128)(2,1)S(1)}, u32[]{:S(2)}, u32[]{:S(2)}) %collective-permute-start.11) | collective-permute-done | bytes 426016 | tf_op jit(solution)/shard_map/ppermute | solution.py:144
  53.9 31.9 %collective-permute-done.refs_1_ = bf16[128,1664]{1,0:T(8,128)(2,1)S(1)} collective-permute-done((bf16[128,1664]{1,0:T(8,128)(2,1)S(1)}, bf16[128,1664]{1,0:T(8,128)(2,1)S(1)}, u32[]{:S(2)}, u32[]{:S(2)}) %collective-permute-start) | collective-permute-done | bytes 426016 | tf_op jit(solution)/shard_map/ppermute | solution.py:139
  87.4 7.7 %collective-permute-done.29 = bf16[128,1536]{1,0:T(8,128)(2,1)S(1)} collective-permute-done((bf16[128,1536]{1,0:T(8,128)(2,1)}, bf16[128,1536]{1,0:T(8,128)(2,1)S(1)}, u32[]{:S(2)}, u32[]{:S(2)}) %collective-permute-start.29) | collective-permute-done | bytes 393248 | tf_op jit(solution)/shard_map/ppermute | solution.py:144
  99.1 5.2 collective-permute-done.2.refs_3_
  105.8 5.8 collective-permute-done.3.refs_4_
  117.9 8.4 %fusion.12 = (bf16[16,1,96,1536]{3,2,1,0:T(8,128)(2,1)}, bf16[16,1,96,1536]{3,2,1,0:T(8,128)(2,1)}) fusion(bf16[16,2,96,1536]{3,2,1,0:T(8,128)(2,1)} %param.11), kind=kLoop, calls=%fused_computation.31 | loop fusion | bytes 18874368 | tf_op jit(solution)/shard_map/slice | solution.py:415
  132.8 15.6 %collective-permute-done.34.refs_3_ = bf16[64,1536]{1,0:T(8,128)(2,1)} collective-permute-done((bf16[64,1536]{1,0:T(8,128)(2,1)}, bf16[64,1536]{1,0:T(8,128)(2,1)}, u32[]{:S(2)}, u32[]{:S(2)}) %collective-permute-start.34) | collective-permute-done | bytes 196640 | tf_op jit(solution)/shard_map/ppermute | solution.py:139
  149.8 9.3 %collective-permute-done.35.refs_4_ = bf16[64,1536]{1,0:T(8,128)(2,1)S(1)} collective-permute-done((bf16[64,1536]{1,0:T(8,128)(2,1)S(1)}, bf16[64,1536]{1,0:T(8,128)(2,1)S(1)}, u32[]{:S(2)}, u32[]{:S(2)}) %collective-permute-start.35) | collective-permute-done | bytes 196640 | tf_op jit(solution)/shard_map/ppermute | solution.py:139
  162.2 20.8 %hidden_and_part.3 = (bf16[1024,1536]{1,0:T(8,128)(2,1)}, bf16[1024,1536]{1,0:T(8,128)(2,1)}) custom-call(bf16[128,1664]{1,0:T(8,128)(2,1)} %copy-done.43, bf16[128,1664]{1,0:T(8,128)(2,1)} %copy-done.51, bf16[128,1664]{1,0:T(8,128)(2,1)} %copy-done.52, bf16[64,1664]{1,0:T(8,128)(2,1)} %copy-done.57, bf16[64,1664]{1,0:T(8,128)(2,1)} %copy-done.58, ...), custom_call_target="tpu_custom_call" | custom-call | flops 9663676416 | bytes 18874368 | tf_op jit(solution)/shard_map/hidden_and_part/pallas_call | solution.py:240
  187.0 27.2 %hidden_and_part.4 = (bf16[1536,1536]{1,0:T(8,128)(2,1)}, bf16[1536,1536]{1,0:T(8,128)(2,1)}) custom-call(bf16[384,1664]{1,0:T(8,128)(2,1)} %constant_dynamic-update-slice_fusion.refs_0_, bf16[384,1664]{1,0:T(8,128)(2,1)} %copy-done.46, bf16[384,1664]{1,0:T(8,128)(2,1)} %collective-permute-done.14.refs_2_, ...), custom_call_target="tpu_custom_call" | custom-call | flops 14495514624 | bytes 23592960 | tf_op jit(solution)/shard_map/hidden_and_part/pallas_call | solution.py:240
  215.5 27.4 %hidden_and_part.5 = (bf16[1536,1536]{1,0:T(8,128)(2,1)}, bf16[1536,1536]{1,0:T(8,128)(2,1)}) custom-call(bf16[384,1664]{1,0:T(8,128)(2,1)} %collective-permute-done.17.refs_0_, bf16[384,1664]{1,0:T(8,128)(2,1)} %collective-permute-done.18.refs_1_, bf16[384,1664]{1,0:T(8,128)(2,1)} %collective-permute-done.19.refs_2_, ...), custom_call_target="tpu_custom_call" | custom-call | flops 14495514624 | bytes 23592960 | tf_op jit(solution)/shard_map/hidden_and_part/pallas_call | solution.py:240
  245.1 13.4 %updated_rows.3 = bf16[384,1536]{1,0:T(8,128)(2,1)} custom-call(bf16[128,1536]{1,0:T(8,128)(2,1)} %fusion.refs_0_, bf16[128,1536]{1,0:T(8,128)(2,1)} %copy-done.30, bf16[128,1536]{1,0:T(8,128)(2,1)} %collective-permute-done.33.refs_2_, bf16[64,1536]{1,0:T(8,128)(2,1)} %collective-permute-done.34.refs_3_, bf16[64,1536]{1,0:T(8,128)(2,1)} %copy-done.48, ...), custom_call_target="tpu_custom_call" | custom-call | flops 4831838208 | bytes 17301504 | tf_op jit(solution)/shard_map/updated_rows/pallas_call | solution.py:310
  259.6 24.1 %updated_rows.2 = bf16[1152,1536]{1,0:T(8,128)(2,1)} custom-call(bf16[128,1536]{1,0:T(8,128)(2,1)} %fusion.refs_0_, bf16[128,1536]{1,0:T(8,128)(2,1)} %copy-done.30, bf16[128,1536]{1,0:T(8,128)(2,1)} %collective-permute-done.33.refs_2_, bf16[64,1536]{1,0:T(8,128)(2,1)} %collective-permute-done.34.refs_3_, bf16[64,1536]{1,0:T(8,128)(2,1)} %copy-done.48, ...), custom_call_target="tpu_custom_call" | custom-call | flops 14495514624 | bytes 26738688 | tf_op jit(solution)/shard_map/updated_rows/pallas_call | solution.py:310
  290.3 23.3 %collective-permute-done.50.refs_1_ = bf16[4,96,1536]{2,1,0:T(8,128)(2,1)S(1)} collective-permute-done((bf16[4,96,1536]{2,1,0:T(8,128)(2,1)S(1)}, bf16[4,96,1536]{2,1,0:T(8,128)(2,1)S(1)}, u32[]{:S(2)}, u32[]{:S(2)}) %collective-permute-start.50) | collective-permute-done | bytes 1179680 | tf_op jit(solution)/shard_map/ppermute | solution.py:139
  317.9 11.1 %collective-permute-done.56.refs_3_ = bf16[2,96,1536]{2,1,0:T(8,128)(2,1)S(1)} collective-permute-done((bf16[2,96,1536]{2,1,0:T(8,128)(2,1)S(1)}, bf16[2,96,1536]{2,1,0:T(8,128)(2,1)S(1)}, u32[]{:S(2)}, u32[]{:S(2)}) %collective-permute-start.56) | collective-permute-done | bytes 589856 | tf_op jit(solution)/shard_map/ppermute | solution.py:139
  330.1 10.1 %collective-permute-done.65.refs_3_ = bf16[2,96,1536]{2,1,0:T(8,128)(2,1)} collective-permute-done((bf16[2,96,1536]{2,1,0:T(8,128)(2,1)S(1)}, bf16[2,96,1536]{2,1,0:T(8,128)(2,1)}, u32[]{:S(2)}, u32[]{:S(2)}) %collective-permute-start.65) | collective-permute-done | bytes 589856 | tf_op jit(solution)/shard_map/ppermute | solution.py:139
  342.3 15.2 %collective-permute-done.52.refs_1_ = bf16[4,96,1536]{2,1,0:T(8,128)(2,1)S(1)} collective-permute-done((bf16[4,96,1536]{2,1,0:T(8,128)(2,1)S(1)}, bf16[4,96,1536]{2,1,0:T(8,128)(2,1)S(1)}, u32[]{:S(2)}, u32[]{:S(2)}) %collective-permute-start.52) | collective-permute-done | bytes 1179680 | tf_op jit(solution)/shard_map/ppermute | solution.py:139
  358.1 8.7 %collective-permute-done.53.refs_2_ = bf16[4,96,1536]{2,1,0:T(8,128)(2,1)} collective-permute-done((bf16[4,96,1536]{2,1,0:T(8,128)(2,1)S(1)}, bf16[4,96,1536]{2,1,0:T(8,128)(2,1)}, u32[]{:S(2)}, u32[]{:S(2)}) %collective-permute-start.53) | collective-permute-done | bytes 1179680 | tf_op jit(solution)/shard_map/ppermute | solution.py:139
  371.1 13.7 %collective-permute-done.77.refs_1_ = bf16[4,96,1536]{2,1,0:T(8,128)(2,1)} collective-permute-done((bf16[4,96,1536]{2,1,0:T(8,128)(2,1)S(1)}, bf16[4,96,1536]{2,1,0:T(8,128)(2,1)}, u32[]{:S(2)}, u32[]{:S(2)}) %collective-permute-start.77) | collective-permute-done | bytes 1179680 | tf_op jit(solution)/shard_map/ppermute | solution.py:139
  385.4 7.1 %collective-permute-done.78.refs_2_ = bf16[4,96,1536]{2,1,0:T(8,128)(2,1)} collective-permute-done((bf16[4,96,1536]{2,1,0:T(8,128)(2,1)S(1)}, bf16[4,96,1536]{2,1,0:T(8,128)(2,1)}, u32[]{:S(2)}, u32[]{:S(2)}) %collective-permute-start.78) | collective-permute-done | bytes 1179680 | tf_op jit(solution)/shard_map/ppermute | solution.py:139
  392.6 7.1 %place.4.refs_10_ = bf16[16,8,96,1536]{3,2,1,0:T(8,128)(2,1)} custom-call(bf16[4,96,1536]{2,1,0:T(8,128)(2,1)} %bitcast.26, bf16[4,96,1536]{2,1,0:T(8,128)(2,1)} %copy-done.9, bf16[4,96,1536]{2,1,0:T(8,128)(2,1)} %copy-done.10, bf16[2,96,1536]{2,1,0:T(8,128)(2,1)} %copy-done.32, bf16[2,96,1536]{2,1,0:T(8,128)(2,1)} %copy-done.33, ...), custom_call_target="tpu_custom_call" | custom-call | tf_op jit(solution)/shard_map/place/pallas_call | solution.py:365
  412.8 3.8 collective-permute-done.71.refs_9_
  423.7 9.4 %collective-permute-done.63.refs_3_ = bf16[2,96,1536]{2,1,0:T(8,128)(2,1)S(1)} collective-permute-done((bf16[2,96,1536]{2,1,0:T(8,128)(2,1)}, bf16[2,96,1536]{2,1,0:T(8,128)(2,1)S(1)}, u32[]{:S(2)}, u32[]{:S(2)}) %collective-permute-start.63) | collective-permute-done | bytes 589856 | tf_op jit(solution)/shard_map/ppermute | solution.py:139
  438.0 7.1 %collective-permute-done.79.refs_3_ = bf16[2,96,1536]{2,1,0:T(8,128)(2,1)S(1)} collective-permute-done((bf16[2,96,1536]{2,1,0:T(8,128)(2,1)}, bf16[2,96,1536]{2,1,0:T(8,128)(2,1)S(1)}, u32[]{:S(2)}, u32[]{:S(2)}) %collective-permute-start.79) | collective-permute-done | bytes 589856 | tf_op jit(solution)/shard_map/ppermute | solution.py:139
  448.2 7.1 %place.5.refs_10_ = bf16[16,8,96,1536]{3,2,1,0:T(8,128)(2,1)} custom-call(bf16[4,96,1536]{2,1,0:T(8,128)(2,1)} %bitcast.44, bf16[4,96,1536]{2,1,0:T(8,128)(2,1)} %copy-done.13, bf16[4,96,1536]{2,1,0:T(8,128)(2,1)} %copy-done.15, bf16[2,96,1536]{2,1,0:T(8,128)(2,1)} %collective-permute-done.65.refs_3_, ...), custom_call_target="tpu_custom_call", output_to_operand_aliasing={{}: (10, {})} | custom-call | tf_op jit(solution)/shard_map/place/pallas_call | solution.py:365
  458.0 12.8 %collective-permute-done.25 = bf16[512,1536]{1,0:T(8,128)(2,1)S(1)} collective-permute-done((bf16[512,1536]{1,0:T(8,128)(2,1)}, bf16[512,1536]{1,0:T(8,128)(2,1)S(1)}, u32[]{:S(2)}, u32[]{:S(2)}) %collective-permute-start.25) | collective-permute-done | bytes 1572896 | tf_op jit(solution)/shard_map/ppermute | solution.py:149
  470.8 100.6 %collective-permute-done.24 = bf16[512,1536]{1,0:T(8,128)(2,1)} collective-permute-done((bf16[512,1536]{1,0:T(8,128)(2,1)}, bf16[512,1536]{1,0:T(8,128)(2,1)}, u32[]{:S(2)}, u32[]{:S(2)}) %collective-permute-start.24) | collective-permute-done | bytes 1572896 | tf_op jit(solution)/shard_map/ppermute | solution.py:149
  572.0 3.9 fusion.11
  579.6 7.1 %place.6.refs_10_ = bf16[16,8,96,1536]{3,2,1,0:T(8,128)(2,1)} custom-call(bf16[4,96,1536]{2,1,0:T(8,128)(2,1)} %bitcast.40, bf16[4,96,1536]{2,1,0:T(8,128)(2,1)} %collective-permute-done.77.refs_1_, bf16[4,96,1536]{2,1,0:T(8,128)(2,1)} %collective-permute-done.78.refs_2_, bf16[2,96,1536]{2,1,0:T(8,128)(2,1)} %copy-done.39, ...), custom_call_target="tpu_custom_call", output_to_operand_aliasing={{}: (10, {})} | custom-call | tf_op jit(solution)/shard_map/place/pallas_call | solution.py:365
  586.8 7.2 %place.7 = bf16[16,8,96,1536]{3,2,1,0:T(8,128)(2,1)} custom-call(bf16[4,96,1536]{2,1,0:T(8,128)(2,1)} %bitcast.36, bf16[4,96,1536]{2,1,0:T(8,128)(2,1)} %copy-done.11, bf16[4,96,1536]{2,1,0:T(8,128)(2,1)} %collective-permute-done.53.refs_2_, bf16[2,96,1536]{2,1,0:T(8,128)(2,1)} %copy-done.37, ...), custom_call_target="tpu_custom_call", output_to_operand_aliasing={{}: (10, {})} | custom-call | tf_op jit(solution)/shard_map/place/pallas_call | solution.py:365
  (319 shorter events, 104.8 us)
Async XLA Ops:
  8.7 36.4 %collective-permute-start.11 = (bf16[128,1664]{1,0:T(8,128)(2,1)S(1)}, bf16[128,1664]{1,0:T(8,128)(2,1)S(1)}, u32[]{:S(2)}, u32[]{:S(2)}) collective-permute-start(bf16[128,1664]{1,0:T(8,128)(2,1)S(1)} %concatenate.9.refs_0_), channel_id=1, source_target_pairs={{4,0},{6,2},{0,4},{2,6},{5,1},{7,3},{1,5},{3,7},{12,8},{14,10},{8,... | collective-permute-start | bytes 1277960 | tf_op jit(solution)/shard_map/ppermute | solution.py:144
  8.7 36.4 %collective-permute-start.12 = (bf16[128,1664]{1,0:T(8,128)(2,1)S(1)}, bf16[128,1664]{1,0:T(8,128)(2,1)S(1)}, u32[]{:S(2)}, u32[]{:S(2)}) collective-permute-start(bf16[128,1664]{1,0:T(8,128)(2,1)S(1)} %concatenate.9.refs_0_), channel_id=1, source_target_pairs={{6,0},{0,2},{2,4},{4,6},{7,1},{1,3},{3,5},{5,7},{14,8},{8,10},{10,... | collective-permute-start | bytes 1277960 | tf_op jit(solution)/shard_map/ppermute | solution.py:144
  47.5 47.8 %collective-permute-start.13 = (bf16[384,1664]{1,0:T(8,128)(2,1)}, bf16[384,1664]{1,0:T(8,128)(2,1)S(1)}, u32[]{:S(2)}, u32[]{:S(2)}) collective-permute-start(bf16[384,1664]{1,0:T(8,128)(2,1)} %constant_dynamic-update-slice_fusion.refs_0_), channel_id=1, source_target_pairs={{0,8},{8,0},{16,24},{24,16},{1,9},{9,1},{17,25},{25,17},{2,10},{10... | collective-permute-start | bytes 3833864 | tf_op jit(solution)/shard_map/ppermute | solution.py:139
  49.0 46.3 %collective-permute-start.14 = (bf16[384,1664]{1,0:T(8,128)(2,1)}, bf16[384,1664]{1,0:T(8,128)(2,1)}, u32[]{:S(2)}, u32[]{:S(2)}) collective-permute-start(bf16[384,1664]{1,0:T(8,128)(2,1)} %constant_dynamic-update-slice_fusion.refs_0_), channel_id=1, source_target_pairs={{0,16},{8,24},{16,0},{24,8},{1,17},{9,25},{17,1},{25,9},{2,18},{10... | collective-permute-start | bytes 3833864 | tf_op jit(solution)/shard_map/ppermute | solution.py:139
  50.5 35.3 %collective-permute-start = (bf16[128,1664]{1,0:T(8,128)(2,1)S(1)}, bf16[128,1664]{1,0:T(8,128)(2,1)S(1)}, u32[]{:S(2)}, u32[]{:S(2)}) collective-permute-start(bf16[128,1664]{1,0:T(8,128)(2,1)S(1)} %concatenate.9.refs_0_), channel_id=1, source_target_pairs={{0,8},{8,0},{16,24},{24,16},{1,9},{9,1},{17,25},{25,17},{2,10},{10... | collective-permute-start | bytes 1277960 | tf_op jit(solution)/shard_map/ppermute | solution.py:139
  51.1 34.8 %collective-permute-start.31 = (bf16[128,1536]{1,0:T(8,128)(2,1)}, bf16[128,1536]{1,0:T(8,128)(2,1)S(1)}, u32[]{:S(2)}, u32[]{:S(2)}) collective-permute-start(bf16[128,1536]{1,0:T(8,128)(2,1)} %fusion.refs_0_), channel_id=1, source_target_pairs={{6,0},{0,2},{2,4},{4,6},{7,1},{1,3},{3,5},{5,7},{14,8},{8,10},{10,... | collective-permute-start | bytes 1179656 | tf_op jit(solution)/shard_map/ppermute | solution.py:144
  51.9 35.5 %collective-permute-start.30 = (bf16[128,1536]{1,0:T(8,128)(2,1)}, bf16[128,1536]{1,0:T(8,128)(2,1)S(1)}, u32[]{:S(2)}, u32[]{:S(2)}) collective-permute-start(bf16[128,1536]{1,0:T(8,128)(2,1)} %fusion.refs_0_), channel_id=1, source_target_pairs={{4,0},{6,2},{0,4},{2,6},{5,1},{7,3},{1,5},{3,7},{12,8},{14,10},{8,... | collective-permute-start | bytes 1179656 | tf_op jit(solution)/shard_map/ppermute | solution.py:144
  113.0 48.7 %collective-permute-start.36 = (bf16[384,1536]{1,0:T(8,128)(2,1)S(1)}, bf16[384,1536]{1,0:T(8,128)(2,1)S(1)}, u32[]{:S(2)}, u32[]{:S(2)}) collective-permute-start(bf16[384,1536]{1,0:T(8,128)(2,1)S(1)} %pad_maximum_fusion.refs_5_), channel_id=1, source_target_pairs={{0,8},{8,0},{16,24},{24,16},{1,9},{9,1},{17,25},{25,17},{2,10},{10... | collective-permute-start | bytes 3538952 | tf_op jit(solution)/shard_map/ppermute | solution.py:139
  115.2 46.6 %collective-permute-start.37 = (bf16[384,1536]{1,0:T(8,128)(2,1)S(1)}, bf16[384,1536]{1,0:T(8,128)(2,1)S(1)}, u32[]{:S(2)}, u32[]{:S(2)}) collective-permute-start(bf16[384,1536]{1,0:T(8,128)(2,1)S(1)} %pad_maximum_fusion.refs_5_), channel_id=1, source_target_pairs={{0,16},{8,24},{16,0},{24,8},{1,17},{9,25},{17,1},{25,9},{2,18},{10... | collective-permute-start | bytes 3538952 | tf_op jit(solution)/shard_map/ppermute | solution.py:139
  117.4 30.9 %collective-permute-start.34 = (bf16[64,1536]{1,0:T(8,128)(2,1)}, bf16[64,1536]{1,0:T(8,128)(2,1)}, u32[]{:S(2)}, u32[]{:S(2)}) collective-permute-start(bf16[64,1536]{1,0:T(8,128)(2,1)} %slice.141), channel_id=1, source_target_pairs={{0,16},{8,24},{16,0},{24,8},{1,17},{9,25},{17,1},{25,9},{2,18},{10... | collective-permute-start | bytes 589832 | tf_op jit(solution)/shard_map/ppermute | solution.py:139
  129.7 31.5 %collective-permute-start.15 = (bf16[192,1664]{1,0:T(8,128)(2,1)S(1)}, bf16[192,1664]{1,0:T(8,128)(2,1)}, u32[]{:S(2)}, u32[]{:S(2)}) collective-permute-start(bf16[192,1664]{1,0:T(8,128)(2,1)S(1)} %slice.132), channel_id=1, source_target_pairs={{0,16},{8,24},{16,0},{24,8},{1,17},{9,25},{17,1},{25,9},{2,18},{10... | collective-permute-start | bytes 1916936 | tf_op jit(solution)/shard_map/ppermute | solution.py:139
  131.3 29.9 %collective-permute-start.16 = (bf16[192,1664]{1,0:T(8,128)(2,1)S(1)}, bf16[192,1664]{1,0:T(8,128)(2,1)S(1)}, u32[]{:S(2)}, u32[]{:S(2)}) collective-permute-start(bf16[192,1664]{1,0:T(8,128)(2,1)S(1)} %slice.133), channel_id=1, source_target_pairs={{0,8},{8,0},{16,24},{24,16},{1,9},{9,1},{17,25},{25,17},{2,10},{10... | collective-permute-start | bytes 1916936 | tf_op jit(solution)/shard_map/ppermute | solution.py:139
  183.2 31.1 %collective-permute-start.19 = (bf16[384,1664]{1,0:T(8,128)(2,1)}, bf16[384,1664]{1,0:T(8,128)(2,1)}, u32[]{:S(2)}, u32[]{:S(2)}) collective-permute-start(bf16[384,1664]{1,0:T(8,128)(2,1)} %collective-permute-done.14.refs_2_), channel_id=1, source_target_pairs={{0,1},{1,0},{2,3},{3,2},{4,5},{5,4},{6,7},{7,6},{8,9},{9,8},{10,11... | collective-permute-start | bytes 3833864 | tf_op jit(solution)/shard_map/ppermute | solution.py:139
  183.5 30.9 %collective-permute-start.20 = (bf16[192,1664]{1,0:T(8,128)(2,1)}, bf16[192,1664]{1,0:T(8,128)(2,1)}, u32[]{:S(2)}, u32[]{:S(2)}) collective-permute-start(bf16[192,1664]{1,0:T(8,128)(2,1)} %collective-permute-done.15.refs_3_), channel_id=1, source_target_pairs={{0,1},{1,0},{2,3},{3,2},{4,5},{5,4},{6,7},{7,6},{8,9},{9,8},{10,11... | collective-permute-start | bytes 1916936 | tf_op jit(solution)/shard_map/ppermute | solution.py:139
  183.7 31.1 %collective-permute-start.21 = (bf16[192,1664]{1,0:T(8,128)(2,1)}, bf16[192,1664]{1,0:T(8,128)(2,1)}, u32[]{:S(2)}, u32[]{:S(2)}) collective-permute-start(bf16[192,1664]{1,0:T(8,128)(2,1)} %copy-done.53), channel_id=1, source_target_pairs={{0,1},{1,0},{2,3},{3,2},{4,5},{5,4},{6,7},{7,6},{8,9},{9,8},{10,11... | collective-permute-start | bytes 1916936 | tf_op jit(solution)/shard_map/ppermute | solution.py:139
  184.0 31.0 %collective-permute-start.38 = (bf16[192,1536]{1,0:T(8,128)(2,1)S(1)}, bf16[192,1536]{1,0:T(8,128)(2,1)}, u32[]{:S(2)}, u32[]{:S(2)}) collective-permute-start(bf16[192,1536]{1,0:T(8,128)(2,1)S(1)} %slice.143), channel_id=1, source_target_pairs={{0,16},{8,24},{16,0},{24,8},{1,17},{9,25},{17,1},{25,9},{2,18},{10... | collective-permute-start | bytes 1769480 | tf_op jit(solution)/shard_map/ppermute | solution.py:139
  185.5 29.9 %collective-permute-start.39 = (bf16[192,1536]{1,0:T(8,128)(2,1)S(1)}, bf16[192,1536]{1,0:T(8,128)(2,1)}, u32[]{:S(2)}, u32[]{:S(2)}) collective-permute-start(bf16[192,1536]{1,0:T(8,128)(2,1)S(1)} %slice.144), channel_id=1, source_target_pairs={{0,8},{8,0},{16,24},{24,16},{1,9},{9,1},{17,25},{25,17},{2,10},{10... | collective-permute-start | bytes 1769480 | tf_op jit(solution)/shard_map/ppermute | solution.py:139
  258.4 30.7 %collective-permute-start.54 = (bf16[4,96,1536]{2,1,0:T(8,128)(2,1)}, bf16[4,96,1536]{2,1,0:T(8,128)(2,1)S(1)}, u32[]{:S(2)}, u32[]{:S(2)}) collective-permute-start(bf16[4,96,1536]{2,1,0:T(8,128)(2,1)} %bitcast.24), channel_id=1, source_target_pairs={{0,8},{8,0},{16,24},{24,16},{1,9},{9,1},{17,25},{25,17},{2,10},{10... | collective-permute-start | bytes 3538952 | tf_op jit(solution)/shard_map/ppermute | solution.py:139
  259.1 30.7 %collective-permute-start.55 = (bf16[4,96,1536]{2,1,0:T(8,128)(2,1)}, bf16[4,96,1536]{2,1,0:T(8,128)(2,1)S(1)}, u32[]{:S(2)}, u32[]{:S(2)}) collective-permute-start(bf16[4,96,1536]{2,1,0:T(8,128)(2,1)} %bitcast.25), channel_id=1, source_target_pairs={{0,16},{8,24},{16,0},{24,8},{1,17},{9,25},{17,1},{25,9},{2,18},{10... | collective-permute-start | bytes 3538952 | tf_op jit(solution)/shard_map/ppermute | solution.py:139
  287.6 28.8 %collective-permute-start.51 = (bf16[4,96,1536]{2,1,0:T(8,128)(2,1)S(1)}, bf16[4,96,1536]{2,1,0:T(8,128)(2,1)S(1)}, u32[]{:S(2)}, u32[]{:S(2)}) collective-permute-start(bf16[4,96,1536]{2,1,0:T(8,128)(2,1)S(1)} %bitcast.42), channel_id=1, source_target_pairs={{0,16},{8,24},{16,0},{24,8},{1,17},{9,25},{17,1},{25,9},{2,18},{10... | collective-permute-start | bytes 3538952 | tf_op jit(solution)/shard_map/ppermute | solution.py:139
  289.1 119.7 %collective-permute-start.22 = (bf16[1536,1536]{1,0:T(8,128)(2,1)}, bf16[1536,1536]{1,0:T(8,128)(2,1)}, u32[]{:S(2)}, u32[]{:S(2)}) collective-permute-start(bf16[1536,1536]{1,0:T(8,128)(2,1)} %get-tuple-element.30), channel_id=1, source_target_pairs={{0,1},{1,0},{2,3},{3,2},{4,5},{5,4},{6,7},{7,6},{8,9},{9,8},{10,11... | collective-permute-start | bytes 14155784 | tf_op jit(solution)/shard_map/ppermute | solution.py:139
  289.1 40.5 %collective-permute-start.58 = (bf16[4,96,1536]{2,1,0:T(8,128)(2,1)S(1)}, bf16[4,96,1536]{2,1,0:T(8,128)(2,1)}, u32[]{:S(2)}, u32[]{:S(2)}) collective-permute-start(bf16[4,96,1536]{2,1,0:T(8,128)(2,1)S(1)} %bitcast.27), channel_id=1, source_target_pairs={{0,1},{1,0},{2,3},{3,2},{4,5},{5,4},{6,7},{7,6},{8,9},{9,8},{10,11... | collective-permute-start | bytes 3538952 | tf_op jit(solution)/shard_map/ppermute | solution.py:139
  289.7 39.3 %collective-permute-start.56 = (bf16[2,96,1536]{2,1,0:T(8,128)(2,1)S(1)}, bf16[2,96,1536]{2,1,0:T(8,128)(2,1)S(1)}, u32[]{:S(2)}, u32[]{:S(2)}) collective-permute-start(bf16[2,96,1536]{2,1,0:T(8,128)(2,1)S(1)} %slice.147), channel_id=1, source_target_pairs={{0,16},{8,24},{16,0},{24,8},{1,17},{9,25},{17,1},{25,9},{2,18},{10... | collective-permute-start | bytes 1769480 | tf_op jit(solution)/shard_map/ppermute | solution.py:139
  369.6 38.0 %collective-permute-start.9 = (bf16[512,1536]{1,0:T(8,128)(2,1)}, bf16[512,1536]{1,0:T(8,128)(2,1)}, u32[]{:S(2)}, u32[]{:S(2)}) collective-permute-start(bf16[512,1536]{1,0:T(8,128)(2,1)} %slice.105), channel_id=1, source_target_pairs={{0,1},{1,0},{2,3},{3,2},{4,5},{5,4},{6,7},{7,6},{8,9},{9,8},{10,11... | collective-permute-start | bytes 4718600 | tf_op jit(solution)/shard_map/ppermute | solution.py:139
  369.7 38.4 %collective-permute-start.67 = (bf16[4,96,1536]{2,1,0:T(8,128)(2,1)S(1)}, bf16[4,96,1536]{2,1,0:T(8,128)(2,1)}, u32[]{:S(2)}, u32[]{:S(2)}) collective-permute-start(bf16[4,96,1536]{2,1,0:T(8,128)(2,1)S(1)} %bitcast.43), channel_id=1, source_target_pairs={{0,1},{1,0},{2,3},{3,2},{4,5},{5,4},{6,7},{7,6},{8,9},{9,8},{10,11... | collective-permute-start | bytes 3538952 | tf_op jit(solution)/shard_map/ppermute | solution.py:139
  421.7 33.7 %collective-permute-start.82 = (bf16[4,96,1536]{2,1,0:T(8,128)(2,1)}, bf16[4,96,1536]{2,1,0:T(8,128)(2,1)}, u32[]{:S(2)}, u32[]{:S(2)}) collective-permute-start(bf16[4,96,1536]{2,1,0:T(8,128)(2,1)} %collective-permute-done.77.refs_1_), channel_id=1, source_target_pairs={{0,1},{1,0},{2,3},{3,2},{4,5},{5,4},{6,7},{7,6},{8,9},{9,8},{10,11... | collective-permute-start | bytes 3538952 | tf_op jit(solution)/shard_map/ppermute | solution.py:139
  433.1 37.7 %collective-permute-start.25 = (bf16[512,1536]{1,0:T(8,128)(2,1)}, bf16[512,1536]{1,0:T(8,128)(2,1)S(1)}, u32[]{:S(2)}, u32[]{:S(2)}) collective-permute-start(bf16[512,1536]{1,0:T(8,128)(2,1)} %get-tuple-element.53), channel_id=1, source_target_pairs={{0,6},{2,0},{4,2},{6,4},{1,7},{3,1},{5,3},{7,5},{8,14},{10,8},{12,... | collective-permute-start | bytes 4718600 | tf_op jit(solution)/shard_map/ppermute | solution.py:149
  435.6 135.8 %collective-permute-start.24 = (bf16[512,1536]{1,0:T(8,128)(2,1)}, bf16[512,1536]{1,0:T(8,128)(2,1)}, u32[]{:S(2)}, u32[]{:S(2)}) collective-permute-start(bf16[512,1536]{1,0:T(8,128)(2,1)} %get-tuple-element.54), channel_id=1, source_target_pairs={{0,4},{2,6},{4,0},{6,2},{1,5},{3,7},{5,1},{7,3},{8,12},{10,14},{12... | collective-permute-start | bytes 4718600 | tf_op jit(solution)/shard_map/ppermute | solution.py:149
  445.1 126.3 %collective-permute-start.23 = (bf16[512,1536]{1,0:T(8,128)(2,1)S(1)}, bf16[512,1536]{1,0:T(8,128)(2,1)}, u32[]{:S(2)}, u32[]{:S(2)}) collective-permute-start(bf16[512,1536]{1,0:T(8,128)(2,1)S(1)} %get-tuple-element.52), channel_id=1, source_target_pairs={{0,2},{2,4},{4,6},{6,0},{1,3},{3,5},{5,7},{7,1},{8,10},{10,12},{12... | collective-permute-start | bytes 4718600 | tf_op jit(solution)/shard_map/ppermute | solution.py:149
  456.0 130.8 %collective-permute-start.73 = (bf16[4,96,1536]{2,1,0:T(8,128)(2,1)S(1)}, bf16[4,96,1536]{2,1,0:T(8,128)(2,1)}, u32[]{:S(2)}, u32[]{:S(2)}) collective-permute-start(bf16[4,96,1536]{2,1,0:T(8,128)(2,1)S(1)} %copy-done.12), channel_id=1, source_target_pairs={{0,1},{1,0},{2,3},{3,2},{4,5},{5,4},{6,7},{7,6},{8,9},{9,8},{10,11... | collective-permute-start | bytes 3538952 | tf_op jit(solution)/shard_map/ppermute | solution.py:139
  457.6 129.2 %collective-permute-start.74 = (bf16[4,96,1536]{2,1,0:T(8,128)(2,1)}, bf16[4,96,1536]{2,1,0:T(8,128)(2,1)}, u32[]{:S(2)}, u32[]{:S(2)}) collective-permute-start(bf16[4,96,1536]{2,1,0:T(8,128)(2,1)} %collective-permute-done.53.refs_2_), channel_id=1, source_target_pairs={{0,1},{1,0},{2,3},{3,2},{4,5},{5,4},{6,7},{7,6},{8,9},{9,8},{10,11... | collective-permute-start | bytes 3538952 | tf_op jit(solution)/shard_map/ppermute | solution.py:139
  470.8 105.3 %collective-permute-start.76 = (bf16[2,96,1536]{2,1,0:T(8,128)(2,1)}, bf16[2,96,1536]{2,1,0:T(8,128)(2,1)S(1)}, u32[]{:S(2)}, u32[]{:S(2)}) collective-permute-start(bf16[2,96,1536]{2,1,0:T(8,128)(2,1)} %copy-done.38), channel_id=1, source_target_pairs={{0,1},{1,0},{2,3},{3,2},{4,5},{5,4},{6,7},{7,6},{8,9},{9,8},{10,11... | collective-permute-start | bytes 1769480 | tf_op jit(solution)/shard_map/ppermute | solution.py:139
  (117 other events, 3001.1 us)

commit v3 on v2

--- a/solution.py
+++ b/solution.py
@@ -475,38 +475,21 @@
     head = updated_rows(noises, layouts, acts, w_down, step_scale, columns, 0, 1)
     rest = updated_rows(noises, layouts, acts, w_down, step_scale, columns, 1, chunks - 1)
     new_down = None
-    waiting = []
     sent = []
     starts = [(0, 0, 0), (0, 1, 0), (0, 2, 0), (0, 3, 0), (chunk // 2, 3, 0)]
     starts += [(offset, bit, 1) for offset, bit, _ in starts]
     for c in range(chunks):
-        last = c == chunks - 1
         mine = head if c == 0 else rest[(c - 1) * columns : c * columns]
         mine = mine.reshape(chunk, units, width)
-
-        def place_next(value):
-            nonlocal new_down
-            n, pieces = waiting.pop(0)
-            new_down = place(new_down, pieces, n * chunk, starts, shape, cores)
-            value, new_down = lax.optimization_barrier((value, new_down))
-            return value
-
         if len(sent) >= 2:
             mine, _ = lax.optimization_barrier((mine, sent[-2]))
         near = plane_neighbours(mine)
         sent.append(near)
+        diagonal = plane_diagonal(*near)
         early = other_core([mine, *near])
-        if last:
-            near = place_next(near)
-        diagonal = plane_diagonal(*near)
-        if last:
-            diagonal = place_next(diagonal)
         late = other_core(diagonal)
-        if last:
-            late = place_next(late)
-        waiting.append((c, [mine, *near, *diagonal, *early, *late]))
-    n, pieces = waiting.pop(0)
-    new_down = place(new_down, pieces, n * chunk, starts, shape, cores)
+        pieces = [mine, *near, *diagonal, *early, *late]
+        new_down = place(new_down, pieces, c * chunk, starts, shape, cores)
     new_down = new_down.reshape(local_experts, hidden_units, width)
     return (moved.astype(jnp.bfloat16).reshape(latents.shape), new_down)
 

time: 598 us -> 586 us (0.980)
  the two profiles are of different devices: /device:TPU:0 before, /device:TPU:8 now
where the time goes in v3:
time: 586 us; the launch traced here: 582 us
  waiting for transfers between devices  327 us (56%)
  Pallas kernels  142 us (24%)
  starting transfers between devices  65.4 us (11%)
  local copies, waits for them, and re-layouts  35.7 us (6%)
  other arithmetic  10 us (2%)
    ppermute x77, waiting for transfers between devices, swap(): lax.ppermute(x, axis, [(i, i ^ bit) for i in range(lax.axis_size(axis))])  192 us
    ppermute x3, waiting for transfers between devices, to_ahead(): return lax.ppermute(x, 'ep', [(i, (i + step) % size) for i in range(size)])  96.8 us
    pallas_call x3, Pallas kernels, hidden_and_part(): pl.pallas_call(lambda *refs: hidden_kernel(*refs, layout=layout, width=wi...  75.7 us
    ppermute x77, starting transfers between devices, swap(): lax.ppermute(x, axis, [(i, i ^ bit) for i in range(lax.axis_size(axis))])  48.1 us
    ppermute x6, waiting for transfers between devices, from_ahead(): return lax.ppermute(x, 'ep', [((i + step) % size, i) for i in range(size)])  38.1 us
    pallas_call x2, Pallas kernels, updated_rows(): pl.pallas_call(lambda *refs: update_kernel(*refs, layouts=layouts, scale=...  37.9 us
    pallas_call x4, Pallas kernels, place(): pl.pallas_call(lambda *refs: place_kernel(*refs, first=first, starts=star...  28.5 us
    ppermute x6, starting transfers between devices, from_ahead(): return lax.ppermute(x, 'ep', [((i + step) % size, i) for i in range(size)])  12 us
  transfers between devices with their start and end apart: 86, of which 28 were waited for; matrix products, arithmetic and copies ran while one was open for 5% of the time, Pallas kernels for 24%

profile of v3, /device:TPU:8, one launch (start us, length us, event | category | flops | bytes accessed | tf_op | source)
XLA Modules:
  0.0 582.0 jit_solution(13279446987276478882)
XLA Ops:
  3.7 3.0 collective-permute-start.11
  10.1 24.5 %collective-permute-done.10 = bf16[128,1664]{1,0:T(8,128)(2,1)S(1)} collective-permute-done((bf16[128,1664]{1,0:T(8,128)(2,1)S(1)}, bf16[128,1664]{1,0:T(8,128)(2,1)S(1)}, u32[]{:S(2)}, u32[]{:S(2)}) %collective-permute-start.10) | collective-permute-done | bytes 426016 | tf_op jit(solution)/shard_map/ppermute | solution.py:144
  34.6 8.3 %collective-permute-done.12 = bf16[128,1664]{1,0:T(8,128)(2,1)S(1)} collective-permute-done((bf16[128,1664]{1,0:T(8,128)(2,1)S(1)}, bf16[128,1664]{1,0:T(8,128)(2,1)S(1)}, u32[]{:S(2)}, u32[]{:S(2)}) %collective-permute-start.12) | collective-permute-done | bytes 426016 | tf_op jit(solution)/shard_map/ppermute | solution.py:144
  50.0 2.8 collective-permute-start.30
  52.8 31.1 %collective-permute-done.refs_1_ = bf16[128,1664]{1,0:T(8,128)(2,1)S(1)} collective-permute-done((bf16[128,1664]{1,0:T(8,128)(2,1)S(1)}, bf16[128,1664]{1,0:T(8,128)(2,1)S(1)}, u32[]{:S(2)}, u32[]{:S(2)}) %collective-permute-start) | collective-permute-done | bytes 426016 | tf_op jit(solution)/shard_map/ppermute | solution.py:139
  88.0 5.3 collective-permute-done.31
  101.4 6.5 %collective-permute-done.3.refs_4_ = bf16[64,1664]{1,0:T(8,128)(2,1)S(1)} collective-permute-done((bf16[64,1664]{1,0:T(8,128)(2,1)S(1)}, bf16[64,1664]{1,0:T(8,128)(2,1)S(1)}, u32[]{:S(2)}, u32[]{:S(2)}) %collective-permute-start.3) | collective-permute-done | bytes 213024 | tf_op jit(solution)/shard_map/ppermute | solution.py:139
  116.5 8.5 %fusion.12 = (bf16[16,1,96,1536]{3,2,1,0:T(8,128)(2,1)}, bf16[16,1,96,1536]{3,2,1,0:T(8,128)(2,1)}) fusion(bf16[16,2,96,1536]{3,2,1,0:T(8,128)(2,1)} %param.11), kind=kLoop, calls=%fused_computation.31 | loop fusion | bytes 18874368 | tf_op jit(solution)/shard_map/slice | solution.py:415
  132.2 14.4 %collective-permute-done.34.refs_3_ = bf16[64,1536]{1,0:T(8,128)(2,1)S(1)} collective-permute-done((bf16[64,1536]{1,0:T(8,128)(2,1)}, bf16[64,1536]{1,0:T(8,128)(2,1)S(1)}, u32[]{:S(2)}, u32[]{:S(2)}) %collective-permute-start.34) | collective-permute-done | bytes 196640 | tf_op jit(solution)/shard_map/ppermute | solution.py:139
  147.5 10.4 %collective-permute-done.35.refs_4_ = bf16[64,1536]{1,0:T(8,128)(2,1)S(1)} collective-permute-done((bf16[64,1536]{1,0:T(8,128)(2,1)S(1)}, bf16[64,1536]{1,0:T(8,128)(2,1)S(1)}, u32[]{:S(2)}, u32[]{:S(2)}) %collective-permute-start.35) | collective-permute-done | bytes 196640 | tf_op jit(solution)/shard_map/ppermute | solution.py:139
  160.3 20.8 %hidden_and_part.3 = (bf16[1024,1536]{1,0:T(8,128)(2,1)}, bf16[1024,1536]{1,0:T(8,128)(2,1)}) custom-call(bf16[128,1664]{1,0:T(8,128)(2,1)} %copy-done.49, bf16[128,1664]{1,0:T(8,128)(2,1)} %copy-done.60, bf16[128,1664]{1,0:T(8,128)(2,1)} %copy-done.61, bf16[64,1664]{1,0:T(8,128)(2,1)} %copy-done.65, bf16[64,1664]{1,0:T(8,128)(2,1)} %copy-done.66, ...), custom_call_target="tpu_custom_call" | custom-call | flops 9663676416 | bytes 18874368 | tf_op jit(solution)/shard_map/hidden_and_part/pallas_call | solution.py:240
  181.1 2.7 slice.105
  189.0 27.3 %hidden_and_part.4 = (bf16[1536,1536]{1,0:T(8,128)(2,1)}, bf16[1536,1536]{1,0:T(8,128)(2,1)}) custom-call(bf16[384,1664]{1,0:T(8,128)(2,1)} %constant_dynamic-update-slice_fusion.refs_0_, bf16[384,1664]{1,0:T(8,128)(2,1)} %copy-done.52, bf16[384,1664]{1,0:T(8,128)(2,1)} %copy-done.54, bf16[192,1664]{1,0:T(8,128)(2,1)} %collective-permute-done.15.refs_3_, ...), custom_call_target="tpu_custom_call" | custom-call | flops 14495514624 | bytes 23592960 | tf_op jit(solution)/shard_map/hidden_and_part/pallas_call | solution.py:240
  217.5 27.7 %hidden_and_part.5 = (bf16[1536,1536]{1,0:T(8,128)(2,1)}, bf16[1536,1536]{1,0:T(8,128)(2,1)}) custom-call(bf16[384,1664]{1,0:T(8,128)(2,1)} %collective-permute-done.17.refs_0_, bf16[384,1664]{1,0:T(8,128)(2,1)} %collective-permute-done.18.refs_1_, bf16[384,1664]{1,0:T(8,128)(2,1)} %collective-permute-done.19.refs_2_, ...), custom_call_target="tpu_custom_call" | custom-call | flops 14495514624 | bytes 23592960 | tf_op jit(solution)/shard_map/hidden_and_part/pallas_call | solution.py:240
  247.5 13.3 %updated_rows.3 = bf16[384,1536]{1,0:T(8,128)(2,1)} custom-call(bf16[128,1536]{1,0:T(8,128)(2,1)} %copy-done.15, bf16[128,1536]{1,0:T(8,128)(2,1)} %copy-done.31, bf16[128,1536]{1,0:T(8,128)(2,1)} %collective-permute-done.33.refs_2_, bf16[64,1536]{1,0:T(8,128)(2,1)} %copy-done.56, bf16[64,1536]{1,0:T(8,128)(2,1)} %copy-done.57, bf16[384,1536]{1,0:T(8,128)(2,1)} %copy-done.1, ...), custom_call_target="tpu_custom_call" | custom-call | flops 4831838208 | bytes 17301504 | tf_op jit(solution)/shard_map/updated_rows/pallas_call | solution.py:310
  262.0 24.5 %updated_rows.2 = bf16[1152,1536]{1,0:T(8,128)(2,1)} custom-call(bf16[128,1536]{1,0:T(8,128)(2,1)} %copy-done.15, bf16[128,1536]{1,0:T(8,128)(2,1)} %copy-done.31, bf16[128,1536]{1,0:T(8,128)(2,1)} %collective-permute-done.33.refs_2_, bf16[64,1536]{1,0:T(8,128)(2,1)} %copy-done.56, bf16[64,1536]{1,0:T(8,128)(2,1)} %copy-done.57, ...), custom_call_target="tpu_custom_call" | custom-call | flops 14495514624 | bytes 26738688 | tf_op jit(solution)/shard_map/updated_rows/pallas_call | solution.py:310
  292.3 24.8 %collective-permute-done.50.refs_1_ = bf16[4,96,1536]{2,1,0:T(8,128)(2,1)S(1)} collective-permute-done((bf16[4,96,1536]{2,1,0:T(8,128)(2,1)S(1)}, bf16[4,96,1536]{2,1,0:T(8,128)(2,1)S(1)}, u32[]{:S(2)}, u32[]{:S(2)}) %collective-permute-start.50) | collective-permute-done | bytes 1179680 | tf_op jit(solution)/shard_map/ppermute | solution.py:139
  321.5 11.8 %collective-permute-done.79.refs_3_ = bf16[2,96,1536]{2,1,0:T(8,128)(2,1)S(1)} collective-permute-done((bf16[2,96,1536]{2,1,0:T(8,128)(2,1)S(1)}, bf16[2,96,1536]{2,1,0:T(8,128)(2,1)S(1)}, u32[]{:S(2)}, u32[]{:S(2)}) %collective-permute-start.79) | collective-permute-done | bytes 589856 | tf_op jit(solution)/shard_map/ppermute | solution.py:139
  335.7 8.7 %collective-permute-done.72.refs_3_ = bf16[2,96,1536]{2,1,0:T(8,128)(2,1)S(1)} collective-permute-done((bf16[2,96,1536]{2,1,0:T(8,128)(2,1)S(1)}, bf16[2,96,1536]{2,1,0:T(8,128)(2,1)S(1)}, u32[]{:S(2)}, u32[]{:S(2)}) %collective-permute-start.72) | collective-permute-done | bytes 589856 | tf_op jit(solution)/shard_map/ppermute | solution.py:139
  350.6 19.3 %collective-permute-done.63.refs_1_ = bf16[4,96,1536]{2,1,0:T(8,128)(2,1)S(1)} collective-permute-done((bf16[4,96,1536]{2,1,0:T(8,128)(2,1)S(1)}, bf16[4,96,1536]{2,1,0:T(8,128)(2,1)S(1)}, u32[]{:S(2)}, u32[]{:S(2)}) %collective-permute-start.63) | collective-permute-done | bytes 1179680 | tf_op jit(solution)/shard_map/ppermute | solution.py:139
  376.6 3.7 add_convert_fusion
  382.9 19.7 %collective-permute-done.52.refs_1_ = bf16[4,96,1536]{2,1,0:T(8,128)(2,1)} collective-permute-done((bf16[4,96,1536]{2,1,0:T(8,128)(2,1)S(1)}, bf16[4,96,1536]{2,1,0:T(8,128)(2,1)}, u32[]{:S(2)}, u32[]{:S(2)}) %collective-permute-start.52) | collective-permute-done | bytes 1179680 | tf_op jit(solution)/shard_map/ppermute | solution.py:139
  402.6 2.5 collective-permute-start.23
  409.1 6.6 %collective-permute-done.65.refs_3_ = bf16[2,96,1536]{2,1,0:T(8,128)(2,1)S(1)} collective-permute-done((bf16[2,96,1536]{2,1,0:T(8,128)(2,1)}, bf16[2,96,1536]{2,1,0:T(8,128)(2,1)S(1)}, u32[]{:S(2)}, u32[]{:S(2)}) %collective-permute-start.65) | collective-permute-done | bytes 589856 | tf_op jit(solution)/shard_map/ppermute | solution.py:139
  417.7 12.6 %collective-permute-done.54.refs_3_ = bf16[2,96,1536]{2,1,0:T(8,128)(2,1)} collective-permute-done((bf16[2,96,1536]{2,1,0:T(8,128)(2,1)S(1)}, bf16[2,96,1536]{2,1,0:T(8,128)(2,1)}, u32[]{:S(2)}, u32[]{:S(2)}) %collective-permute-start.54) | collective-permute-done | bytes 589856 | tf_op jit(solution)/shard_map/ppermute | solution.py:139
  430.9 13.2 %collective-permute-done.55.refs_4_ = bf16[2,96,1536]{2,1,0:T(8,128)(2,1)} collective-permute-done((bf16[2,96,1536]{2,1,0:T(8,128)(2,1)S(1)}, bf16[2,96,1536]{2,1,0:T(8,128)(2,1)}, u32[]{:S(2)}, u32[]{:S(2)}) %collective-permute-start.55) | collective-permute-done | bytes 589856 | tf_op jit(solution)/shard_map/ppermute | solution.py:139
  444.5 62.7 %collective-permute-done.23 = bf16[512,1536]{1,0:T(8,128)(2,1)S(1)} collective-permute-done((bf16[512,1536]{1,0:T(8,128)(2,1)S(1)}, bf16[512,1536]{1,0:T(8,128)(2,1)S(1)}, u32[]{:S(2)}, u32[]{:S(2)}) %collective-permute-start.23) | collective-permute-done | bytes 1572896 | tf_op jit(solution)/shard_map/ppermute | solution.py:149
  507.3 31.7 %collective-permute-done.24 = bf16[512,1536]{1,0:T(8,128)(2,1)S(1)} collective-permute-done((bf16[512,1536]{1,0:T(8,128)(2,1)S(1)}, bf16[512,1536]{1,0:T(8,128)(2,1)S(1)}, u32[]{:S(2)}, u32[]{:S(2)}) %collective-permute-start.24) | collective-permute-done | bytes 1572896 | tf_op jit(solution)/shard_map/ppermute | solution.py:149
  549.2 7.1 %place.4.refs_10_ = bf16[16,8,96,1536]{3,2,1,0:T(8,128)(2,1)} custom-call(bf16[4,96,1536]{2,1,0:T(8,128)(2,1)} %bitcast.26, bf16[4,96,1536]{2,1,0:T(8,128)(2,1)} %copy-done.6, bf16[4,96,1536]{2,1,0:T(8,128)(2,1)} %copy-done.7, bf16[2,96,1536]{2,1,0:T(8,128)(2,1)} %copy-done.32, bf16[2,96,1536]{2,1,0:T(8,128)(2,1)} %copy-done.33, ...), custom_call_target="tpu_custom_call" | custom-call | tf_op jit(solution)/shard_map/place/pallas_call | solution.py:365
  556.4 7.1 %place.5.refs_10_ = bf16[16,8,96,1536]{3,2,1,0:T(8,128)(2,1)} custom-call(bf16[4,96,1536]{2,1,0:T(8,128)(2,1)} %bitcast.44, bf16[4,96,1536]{2,1,0:T(8,128)(2,1)} %copy-done.9, bf16[4,96,1536]{2,1,0:T(8,128)(2,1)} %copy-done.10, bf16[2,96,1536]{2,1,0:T(8,128)(2,1)} %copy-done.39, bf16[2,96,1536]{2,1,0:T(8,128)(2,1)} %copy-done.40, ...), custom_call_target="tpu_custom_call", output_to_operand_aliasing={{}: (10, {})} | custom-call | tf_op jit(solution)/shard_map/place/pallas_call | solution.py:365
  563.5 7.1 %place.6.refs_10_ = bf16[16,8,96,1536]{3,2,1,0:T(8,128)(2,1)} custom-call(bf16[4,96,1536]{2,1,0:T(8,128)(2,1)} %bitcast.40, bf16[4,96,1536]{2,1,0:T(8,128)(2,1)} %copy-done.11, bf16[4,96,1536]{2,1,0:T(8,128)(2,1)} %copy-done.13, bf16[2,96,1536]{2,1,0:T(8,128)(2,1)} %copy-done.43, bf16[2,96,1536]{2,1,0:T(8,128)(2,1)} %copy-done.44, ...), custom_call_target="tpu_custom_call", output_to_operand_aliasing={{}: (10, {})} | custom-call | tf_op jit(solution)/shard_map/place/pallas_call | solution.py:365
  572.5 7.1 %place.7 = bf16[16,8,96,1536]{3,2,1,0:T(8,128)(2,1)} custom-call(bf16[4,96,1536]{2,1,0:T(8,128)(2,1)} %bitcast.36, bf16[4,96,1536]{2,1,0:T(8,128)(2,1)} %collective-permute-done.52.refs_1_, bf16[4,96,1536]{2,1,0:T(8,128)(2,1)} %collective-permute-done.53.refs_2_, ...), custom_call_target="tpu_custom_call", output_to_operand_aliasing={{}: (10, {})} | custom-call | tf_op jit(solution)/shard_map/place/pallas_call | solution.py:365
  (335 shorter events, 103.2 us)
Async XLA Ops:
  3.6 31.0 %collective-permute-start.10 = (bf16[128,1664]{1,0:T(8,128)(2,1)S(1)}, bf16[128,1664]{1,0:T(8,128)(2,1)S(1)}, u32[]{:S(2)}, u32[]{:S(2)}) collective-permute-start(bf16[128,1664]{1,0:T(8,128)(2,1)S(1)} %concatenate.9.refs_0_), channel_id=1, source_target_pairs={{2,0},{4,2},{6,4},{0,6},{3,1},{5,3},{7,5},{1,7},{10,8},{12,10},{14... | collective-permute-start | bytes 1277960 | tf_op jit(solution)/shard_map/ppermute | solution.py:144
  3.7 30.9 %collective-permute-start.11 = (bf16[128,1664]{1,0:T(8,128)(2,1)S(1)}, bf16[128,1664]{1,0:T(8,128)(2,1)S(1)}, u32[]{:S(2)}, u32[]{:S(2)}) collective-permute-start(bf16[128,1664]{1,0:T(8,128)(2,1)S(1)} %concatenate.9.refs_0_), channel_id=1, source_target_pairs={{4,0},{6,2},{0,4},{2,6},{5,1},{7,3},{1,5},{3,7},{12,8},{14,10},{8,... | collective-permute-start | bytes 1277960 | tf_op jit(solution)/shard_map/ppermute | solution.py:144
  6.7 36.2 %collective-permute-start.12 = (bf16[128,1664]{1,0:T(8,128)(2,1)S(1)}, bf16[128,1664]{1,0:T(8,128)(2,1)S(1)}, u32[]{:S(2)}, u32[]{:S(2)}) collective-permute-start(bf16[128,1664]{1,0:T(8,128)(2,1)S(1)} %concatenate.9.refs_0_), channel_id=1, source_target_pairs={{6,0},{0,2},{2,4},{4,6},{7,1},{1,3},{3,5},{5,7},{14,8},{8,10},{10,... | collective-permute-start | bytes 1277960 | tf_op jit(solution)/shard_map/ppermute | solution.py:144
  45.3 49.7 %collective-permute-start.13 = (bf16[384,1664]{1,0:T(8,128)(2,1)}, bf16[384,1664]{1,0:T(8,128)(2,1)S(1)}, u32[]{:S(2)}, u32[]{:S(2)}) collective-permute-start(bf16[384,1664]{1,0:T(8,128)(2,1)} %constant_dynamic-update-slice_fusion.refs_0_), channel_id=1, source_target_pairs={{0,8},{8,0},{16,24},{24,16},{1,9},{9,1},{17,25},{25,17},{2,10},{10... | collective-permute-start | bytes 3833864 | tf_op jit(solution)/shard_map/ppermute | solution.py:139
  46.8 48.2 %collective-permute-start.14 = (bf16[384,1664]{1,0:T(8,128)(2,1)}, bf16[384,1664]{1,0:T(8,128)(2,1)S(1)}, u32[]{:S(2)}, u32[]{:S(2)}) collective-permute-start(bf16[384,1664]{1,0:T(8,128)(2,1)} %constant_dynamic-update-slice_fusion.refs_0_), channel_id=1, source_target_pairs={{0,16},{8,24},{16,0},{24,8},{1,17},{9,25},{17,1},{25,9},{2,18},{10... | collective-permute-start | bytes 3833864 | tf_op jit(solution)/shard_map/ppermute | solution.py:139
  48.3 35.6 %collective-permute-start = (bf16[128,1664]{1,0:T(8,128)(2,1)S(1)}, bf16[128,1664]{1,0:T(8,128)(2,1)S(1)}, u32[]{:S(2)}, u32[]{:S(2)}) collective-permute-start(bf16[128,1664]{1,0:T(8,128)(2,1)S(1)} %concatenate.9.refs_0_), channel_id=1, source_target_pairs={{0,8},{8,0},{16,24},{24,16},{1,9},{9,1},{17,25},{25,17},{2,10},{10... | collective-permute-start | bytes 1277960 | tf_op jit(solution)/shard_map/ppermute | solution.py:139
  48.9 37.5 %collective-permute-start.29 = (bf16[128,1536]{1,0:T(8,128)(2,1)S(1)}, bf16[128,1536]{1,0:T(8,128)(2,1)S(1)}, u32[]{:S(2)}, u32[]{:S(2)}) collective-permute-start(bf16[128,1536]{1,0:T(8,128)(2,1)S(1)} %fusion.refs_0_), channel_id=1, source_target_pairs={{2,0},{4,2},{6,4},{0,6},{3,1},{5,3},{7,5},{1,7},{10,8},{12,10},{14... | collective-permute-start | bytes 1179656 | tf_op jit(solution)/shard_map/ppermute | solution.py:144
  50.0 37.9 %collective-permute-start.30 = (bf16[128,1536]{1,0:T(8,128)(2,1)S(1)}, bf16[128,1536]{1,0:T(8,128)(2,1)S(1)}, u32[]{:S(2)}, u32[]{:S(2)}) collective-permute-start(bf16[128,1536]{1,0:T(8,128)(2,1)S(1)} %fusion.refs_0_), channel_id=1, source_target_pairs={{4,0},{6,2},{0,4},{2,6},{5,1},{7,3},{1,5},{3,7},{12,8},{14,10},{8,... | collective-permute-start | bytes 1179656 | tf_op jit(solution)/shard_map/ppermute | solution.py:144
  112.0 47.8 %collective-permute-start.36 = (bf16[384,1536]{1,0:T(8,128)(2,1)S(1)}, bf16[384,1536]{1,0:T(8,128)(2,1)S(1)}, u32[]{:S(2)}, u32[]{:S(2)}) collective-permute-start(bf16[384,1536]{1,0:T(8,128)(2,1)S(1)} %pad_maximum_fusion.refs_5_), channel_id=1, source_target_pairs={{0,8},{8,0},{16,24},{24,16},{1,9},{9,1},{17,25},{25,17},{2,10},{10... | collective-permute-start | bytes 3538952 | tf_op jit(solution)/shard_map/ppermute | solution.py:139
  113.5 46.3 %collective-permute-start.37 = (bf16[384,1536]{1,0:T(8,128)(2,1)S(1)}, bf16[384,1536]{1,0:T(8,128)(2,1)}, u32[]{:S(2)}, u32[]{:S(2)}) collective-permute-start(bf16[384,1536]{1,0:T(8,128)(2,1)S(1)} %pad_maximum_fusion.refs_5_), channel_id=1, source_target_pairs={{0,16},{8,24},{16,0},{24,8},{1,17},{9,25},{17,1},{25,9},{2,18},{10... | collective-permute-start | bytes 3538952 | tf_op jit(solution)/shard_map/ppermute | solution.py:139
  115.9 30.6 %collective-permute-start.34 = (bf16[64,1536]{1,0:T(8,128)(2,1)}, bf16[64,1536]{1,0:T(8,128)(2,1)S(1)}, u32[]{:S(2)}, u32[]{:S(2)}) collective-permute-start(bf16[64,1536]{1,0:T(8,128)(2,1)} %slice.141), channel_id=1, source_target_pairs={{0,16},{8,24},{16,0},{24,8},{1,17},{9,25},{17,1},{25,9},{2,18},{10... | collective-permute-start | bytes 589832 | tf_op jit(solution)/shard_map/ppermute | solution.py:139
  128.3 30.9 %collective-permute-start.15 = (bf16[192,1664]{1,0:T(8,128)(2,1)S(1)}, bf16[192,1664]{1,0:T(8,128)(2,1)}, u32[]{:S(2)}, u32[]{:S(2)}) collective-permute-start(bf16[192,1664]{1,0:T(8,128)(2,1)S(1)} %slice.132), channel_id=1, source_target_pairs={{0,16},{8,24},{16,0},{24,8},{1,17},{9,25},{17,1},{25,9},{2,18},{10... | collective-permute-start | bytes 1916936 | tf_op jit(solution)/shard_map/ppermute | solution.py:139
  185.3 31.0 %collective-permute-start.19 = (bf16[384,1664]{1,0:T(8,128)(2,1)S(1)}, bf16[384,1664]{1,0:T(8,128)(2,1)}, u32[]{:S(2)}, u32[]{:S(2)}) collective-permute-start(bf16[384,1664]{1,0:T(8,128)(2,1)S(1)} %copy-done.55), channel_id=1, source_target_pairs={{0,1},{1,0},{2,3},{3,2},{4,5},{5,4},{6,7},{7,6},{8,9},{9,8},{10,11... | collective-permute-start | bytes 3833864 | tf_op jit(solution)/shard_map/ppermute | solution.py:139
  185.4 31.0 %collective-permute-start.20 = (bf16[192,1664]{1,0:T(8,128)(2,1)}, bf16[192,1664]{1,0:T(8,128)(2,1)}, u32[]{:S(2)}, u32[]{:S(2)}) collective-permute-start(bf16[192,1664]{1,0:T(8,128)(2,1)} %collective-permute-done.15.refs_3_), channel_id=1, source_target_pairs={{0,1},{1,0},{2,3},{3,2},{4,5},{5,4},{6,7},{7,6},{8,9},{9,8},{10,11... | collective-permute-start | bytes 1916936 | tf_op jit(solution)/shard_map/ppermute | solution.py:139
  185.8 31.1 %collective-permute-start.21 = (bf16[192,1664]{1,0:T(8,128)(2,1)}, bf16[192,1664]{1,0:T(8,128)(2,1)}, u32[]{:S(2)}, u32[]{:S(2)}) collective-permute-start(bf16[192,1664]{1,0:T(8,128)(2,1)} %collective-permute-done.16.refs_4_), channel_id=1, source_target_pairs={{0,1},{1,0},{2,3},{3,2},{4,5},{5,4},{6,7},{7,6},{8,9},{9,8},{10,11... | collective-permute-start | bytes 1916936 | tf_op jit(solution)/shard_map/ppermute | solution.py:139
  186.0 31.0 %collective-permute-start.38 = (bf16[192,1536]{1,0:T(8,128)(2,1)S(1)}, bf16[192,1536]{1,0:T(8,128)(2,1)S(1)}, u32[]{:S(2)}, u32[]{:S(2)}) collective-permute-start(bf16[192,1536]{1,0:T(8,128)(2,1)S(1)} %slice.143), channel_id=1, source_target_pairs={{0,16},{8,24},{16,0},{24,8},{1,17},{9,25},{17,1},{25,9},{2,18},{10... | collective-permute-start | bytes 1769480 | tf_op jit(solution)/shard_map/ppermute | solution.py:139
  245.2 44.9 %collective-permute-start.9 = (bf16[512,1536]{1,0:T(8,128)(2,1)}, bf16[512,1536]{1,0:T(8,128)(2,1)}, u32[]{:S(2)}, u32[]{:S(2)}) collective-permute-start(bf16[512,1536]{1,0:T(8,128)(2,1)} %slice.105), channel_id=1, source_target_pairs={{0,1},{1,0},{2,3},{3,2},{4,5},{5,4},{6,7},{7,6},{8,9},{9,8},{10,11... | collective-permute-start | bytes 4718600 | tf_op jit(solution)/shard_map/ppermute | solution.py:139
  245.7 130.0 %collective-permute-start.22 = (bf16[1536,1536]{1,0:T(8,128)(2,1)}, bf16[1536,1536]{1,0:T(8,128)(2,1)}, u32[]{:S(2)}, u32[]{:S(2)}) collective-permute-start(bf16[1536,1536]{1,0:T(8,128)(2,1)} %get-tuple-element.21), channel_id=1, source_target_pairs={{0,1},{1,0},{2,3},{3,2},{4,5},{5,4},{6,7},{7,6},{8,9},{9,8},{10,11... | collective-permute-start | bytes 14155784 | tf_op jit(solution)/shard_map/ppermute | solution.py:139
  260.9 30.8 %collective-permute-start.61 = (bf16[4,96,1536]{2,1,0:T(8,128)(2,1)}, bf16[4,96,1536]{2,1,0:T(8,128)(2,1)S(1)}, u32[]{:S(2)}, u32[]{:S(2)}) collective-permute-start(bf16[4,96,1536]{2,1,0:T(8,128)(2,1)} %bitcast.24), channel_id=1, source_target_pairs={{0,8},{8,0},{16,24},{24,16},{1,9},{9,1},{17,25},{25,17},{2,10},{10... | collective-permute-start | bytes 3538952 | tf_op jit(solution)/shard_map/ppermute | solution.py:139
  334.2 35.6 %collective-permute-start.63 = (bf16[4,96,1536]{2,1,0:T(8,128)(2,1)S(1)}, bf16[4,96,1536]{2,1,0:T(8,128)(2,1)S(1)}, u32[]{:S(2)}, u32[]{:S(2)}) collective-permute-start(bf16[4,96,1536]{2,1,0:T(8,128)(2,1)S(1)} %bitcast.37), channel_id=1, source_target_pairs={{0,8},{8,0},{16,24},{24,16},{1,9},{9,1},{17,25},{25,17},{2,10},{10... | collective-permute-start | bytes 3538952 | tf_op jit(solution)/shard_map/ppermute | solution.py:139
  375.6 31.4 %collective-permute-start.56 = (bf16[4,96,1536]{2,1,0:T(8,128)(2,1)S(1)}, bf16[4,96,1536]{2,1,0:T(8,128)(2,1)}, u32[]{:S(2)}, u32[]{:S(2)}) collective-permute-start(bf16[4,96,1536]{2,1,0:T(8,128)(2,1)S(1)} %bitcast.35), channel_id=1, source_target_pairs={{0,1},{1,0},{2,3},{3,2},{4,5},{5,4},{6,7},{7,6},{8,9},{9,8},{10,11... | collective-permute-start | bytes 3538952 | tf_op jit(solution)/shard_map/ppermute | solution.py:139
  380.4 35.3 %collective-permute-start.65 = (bf16[2,96,1536]{2,1,0:T(8,128)(2,1)}, bf16[2,96,1536]{2,1,0:T(8,128)(2,1)S(1)}, u32[]{:S(2)}, u32[]{:S(2)}) collective-permute-start(bf16[2,96,1536]{2,1,0:T(8,128)(2,1)} %slice.150), channel_id=1, source_target_pairs={{0,16},{8,24},{16,0},{24,8},{1,17},{9,25},{17,1},{25,9},{2,18},{10... | collective-permute-start | bytes 1769480 | tf_op jit(solution)/shard_map/ppermute | solution.py:139
  382.0 34.4 %collective-permute-start.66 = (bf16[2,96,1536]{2,1,0:T(8,128)(2,1)}, bf16[2,96,1536]{2,1,0:T(8,128)(2,1)S(1)}, u32[]{:S(2)}, u32[]{:S(2)}) collective-permute-start(bf16[2,96,1536]{2,1,0:T(8,128)(2,1)} %slice.151), channel_id=1, source_target_pairs={{0,8},{8,0},{16,24},{24,16},{1,9},{9,1},{17,25},{25,17},{2,10},{10... | collective-permute-start | bytes 1769480 | tf_op jit(solution)/shard_map/ppermute | solution.py:139
  402.6 104.7 %collective-permute-start.23 = (bf16[512,1536]{1,0:T(8,128)(2,1)S(1)}, bf16[512,1536]{1,0:T(8,128)(2,1)S(1)}, u32[]{:S(2)}, u32[]{:S(2)}) collective-permute-start(bf16[512,1536]{1,0:T(8,128)(2,1)S(1)} %get-tuple-element.34), channel_id=1, source_target_pairs={{0,2},{2,4},{4,6},{6,0},{1,3},{3,5},{5,7},{7,1},{8,10},{10,12},{12... | collective-permute-start | bytes 4718600 | tf_op jit(solution)/shard_map/ppermute | solution.py:149
  405.1 133.9 %collective-permute-start.24 = (bf16[512,1536]{1,0:T(8,128)(2,1)S(1)}, bf16[512,1536]{1,0:T(8,128)(2,1)S(1)}, u32[]{:S(2)}, u32[]{:S(2)}) collective-permute-start(bf16[512,1536]{1,0:T(8,128)(2,1)S(1)} %get-tuple-element.36), channel_id=1, source_target_pairs={{0,4},{2,6},{4,0},{6,2},{1,5},{3,7},{5,1},{7,3},{8,12},{10,14},{12... | collective-permute-start | bytes 4718600 | tf_op jit(solution)/shard_map/ppermute | solution.py:149
  407.0 134.3 %collective-permute-start.25 = (bf16[512,1536]{1,0:T(8,128)(2,1)S(1)}, bf16[512,1536]{1,0:T(8,128)(2,1)S(1)}, u32[]{:S(2)}, u32[]{:S(2)}) collective-permute-start(bf16[512,1536]{1,0:T(8,128)(2,1)S(1)} %get-tuple-element.35), channel_id=1, source_target_pairs={{0,6},{2,0},{4,2},{6,4},{1,7},{3,1},{5,3},{7,5},{8,14},{10,8},{12,... | collective-permute-start | bytes 4718600 | tf_op jit(solution)/shard_map/ppermute | solution.py:149
  444.0 99.8 %collective-permute-start.69 = (bf16[4,96,1536]{2,1,0:T(8,128)(2,1)S(1)}, bf16[4,96,1536]{2,1,0:T(8,128)(2,1)S(1)}, u32[]{:S(2)}, u32[]{:S(2)}) collective-permute-start(bf16[4,96,1536]{2,1,0:T(8,128)(2,1)S(1)} %copy-done.14), channel_id=1, source_target_pairs={{0,1},{1,0},{2,3},{3,2},{4,5},{5,4},{6,7},{7,6},{8,9},{9,8},{10,11... | collective-permute-start | bytes 3538952 | tf_op jit(solution)/shard_map/ppermute | solution.py:139
  444.0 100.4 %collective-permute-start.57 = (bf16[4,96,1536]{2,1,0:T(8,128)(2,1)}, bf16[4,96,1536]{2,1,0:T(8,128)(2,1)S(1)}, u32[]{:S(2)}, u32[]{:S(2)}) collective-permute-start(bf16[4,96,1536]{2,1,0:T(8,128)(2,1)} %collective-permute-done.52.refs_1_), channel_id=1, source_target_pairs={{0,1},{1,0},{2,3},{3,2},{4,5},{5,4},{6,7},{7,6},{8,9},{9,8},{10,11... | collective-permute-start | bytes 3538952 | tf_op jit(solution)/shard_map/ppermute | solution.py:139
  507.3 37.6 %collective-permute-start.58 = (bf16[4,96,1536]{2,1,0:T(8,128)(2,1)}, bf16[4,96,1536]{2,1,0:T(8,128)(2,1)}, u32[]{:S(2)}, u32[]{:S(2)}) collective-permute-start(bf16[4,96,1536]{2,1,0:T(8,128)(2,1)} %collective-permute-done.53.refs_2_), channel_id=1, source_target_pairs={{0,1},{1,0},{2,3},{3,2},{4,5},{5,4},{6,7},{7,6},{8,9},{9,8},{10,11... | collective-permute-start | bytes 3538952 | tf_op jit(solution)/shard_map/ppermute | solution.py:139
  544.9 34.7 %collective-permute-start.26 = (bf16[128,1536]{1,0:T(8,128)(2,1)S(1)}, bf16[128,1536]{1,0:T(8,128)(2,1)S(1)}, u32[]{:S(2)}, u32[]{:S(2)}) collective-permute-start(bf16[128,1536]{1,0:T(8,128)(2,1)S(1)} %get-tuple-element.40), channel_id=1, source_target_pairs={{0,8},{8,0},{16,24},{24,16},{1,9},{9,1},{17,25},{25,17},{2,10},{10... | collective-permute-start | bytes 1179656 | tf_op jit(solution)/shard_map/ppermute | solution.py:139
  545.5 34.1 %collective-permute-start.27 = (bf16[128,1536]{1,0:T(8,128)(2,1)S(1)}, bf16[128,1536]{1,0:T(8,128)(2,1)S(1)}, u32[]{:S(2)}, u32[]{:S(2)}) collective-permute-start(bf16[128,1536]{1,0:T(8,128)(2,1)S(1)} %get-tuple-element.42), channel_id=1, source_target_pairs={{0,16},{8,24},{16,0},{24,8},{1,17},{9,25},{17,1},{25,9},{2,18},{10... | collective-permute-start | bytes 1179656 | tf_op jit(solution)/shard_map/ppermute | solution.py:139
  547.8 31.8 %collective-permute-start.28 = (bf16[128,1536]{1,0:T(8,128)(2,1)S(1)}, bf16[128,1536]{1,0:T(8,128)(2,1)}, u32[]{:S(2)}, u32[]{:S(2)}) collective-permute-start(bf16[128,1536]{1,0:T(8,128)(2,1)S(1)} %get-tuple-element.41), channel_id=1, source_target_pairs={{0,24},{8,16},{16,8},{24,0},{1,25},{9,17},{17,9},{25,1},{2,26},{10... | collective-permute-start | bytes 1179656 | tf_op jit(solution)/shard_map/ppermute | solution.py:139
  (125 other events, 3394.2 us)
